TPU v7x, 8 devices: a whole 2x2x1 slice. The times are simulated.
8 devices in a mesh: dp: 2 (over z, y), tp: 4 (over x, core).
Axes of the slice: x: 2, y: 2, z: 1, core: 2. Of those that a mesh axis runs over, the one named last changes fastest.
Arguments:
- x: bfloat16 [4096, 2048], P('dp'), parts along dimension 0
- mu1: float32 [4096], P('dp'), parts along dimension 0
- rs1: float32 [4096], P('dp'), parts along dimension 0
- g1: bfloat16 [2048], replicated
- g2: bfloat16 [2048], replicated
- dy: bfloat16 [4096, 2048], P('dp'), parts along dimension 0
- wqkv: bfloat16 [2048, 6144], P(None, 'tp')
- wo: bfloat16 [32, 64, 2048], P('tp')
- w1: bfloat16 [2048, 8192], P(None, 'tp')
- w2: bfloat16 [8192, 2048], P('tp')
Outputs:
- output 1: bfloat16 [4096, 2048], P('dp'), parts along dimension 0
- output 2: bfloat16 [4096, 6144], P('dp', 'tp'), parts along dimension 0
- output 3: bfloat16 [64, 64, 2048], P(('dp', 'tp')), parts along dimension 0
- output 4: bfloat16 [4096, 8192], P('dp', 'tp'), parts along dimension 0
- output 5: bfloat16 [16384, 2048], P(('dp', 'tp')), parts along dimension 0
There are 2 independent parts. A program takes and returns all parts, laid end to end along the dimension named above; an argument that names none is the same for every part.
All inputs are finite; a program needn't handle non-finite values.
Results may differ from a plain program's by a relative error of at most 0.0158731.
Values are sent between devices in bfloat16 or wider.
A program may use at most 1 GiB of HBM per device.

v0:
```python
import functools

import jax
import jax.numpy as jnp
from jax import lax
from jax.experimental import pallas as pl
from jax.experimental.pallas import tpu as pltpu
from jax.sharding import PartitionSpec as P


EPS = 1.0 / 100000
LOG2E = 1.4426950408889634
f32 = jnp.float32
bf = jnp.bfloat16
NB = 2
BQ = 256
TILE = 256
MB = 2**20
SAME = [(0, 1), (1, 0), (2, 3), (3, 2)]
CROSS = [(0, 2), (2, 0), (1, 3), (3, 1)]


def _dot(a, b):
    return jnp.dot(a, b, preferred_element_type=f32)


def _dot_t(a, b):
    return lax.dot_general(a, b, (((1,), (1,)), ((), ())), preferred_element_type=f32)


def _causal(n):
    return lax.broadcasted_iota(jnp.int32, (n, n), 0) >= lax.broadcasted_iota(jnp.int32, (n, n), 1)


def _params(mb=60):
    return pltpu.CompilerParams(vmem_limit_bytes=mb * MB)


def _cost(flops, nbytes):
    return pl.CostEstimate(flops=int(flops), bytes_accessed=int(nbytes), transcendentals=0)


def _fwd_kernel(*refs, t, hd, first):
    qkv_ref = refs[0]
    o_ref, ofull_ref, lse_ref, tr_ref = refs[1:] if first else refs[4:]
    c = LOG2E * hd**-0.5
    for i in range(t // BQ):
        w = (i + 1) * BQ
        rows = slice(i * BQ, w)
        blk = qkv_ref[rows, :]
        tr_ref[0, :, rows] = blk.T
        scores = []
        for h in range(2):
            q = blk[:, 3 * hd * h : 3 * hd * h + hd]
            kt = slice(3 * hd * h + hd, 3 * hd * h + 2 * hd)
            s = _dot(q, tr_ref[0, kt, :w])
            d = jnp.where(_causal(BQ), s[:, w - BQ :], -jnp.inf)
            scores.append(jnp.concatenate([s[:, : w - BQ], d], 1) if i else d)
        cols, ps = [], []
        for s in scores:
            m = jnp.max(s, axis=1, keepdims=True)
            p = jnp.exp2((s - m) * c)
            l = jnp.sum(p, axis=1, keepdims=True)
            cols += [m * c + jnp.log2(l), 1.0 / l]
            ps.append(p.astype(bf))
        st = jnp.concatenate(cols, 1).T
        outs = []
        for h in range(2):
            vt = slice(3 * hd * h + 2 * hd, 3 * hd * h + 3 * hd)
            outs.append((_dot_t(tr_ref[0, vt, :w], ps[h]) * st[2 * h + 1 : 2 * h + 2]).astype(bf))
            lse_ref[0, h : h + 1, rows] = st[2 * h : 2 * h + 1]
        o = jnp.concatenate(outs, 0).T
        o_ref[rows, :] = o
        ofull_ref[rows, :] = o


def _attn_fwd(qkv, hd, start, npair, prev):
    t, w = qkv.shape
    total = w // (6 * hd)
    full = [jax.ShapeDtypeStruct((t, total * 2 * hd), bf), jax.ShapeDtypeStruct((total, 2, t), f32), jax.ShapeDtypeStruct((total, 6 * hd, t), bf)]
    return pl.pallas_call(
        functools.partial(_fwd_kernel, t=t, hd=hd, first=prev is None),
        grid=(npair,),
        in_specs=[pl.BlockSpec((t, 6 * hd), lambda p: (0, p + start))] + ([] if prev is None else [pl.BlockSpec(memory_space=pl.ANY)] * 3),
        out_specs=[
            pl.BlockSpec((t, 2 * hd), lambda p: (0, p)),
            pl.BlockSpec((t, 2 * hd), lambda p: (0, p + start)),
            pl.BlockSpec((1, 2, t), lambda p: (p + start, 0, 0)),
            pl.BlockSpec((1, 6 * hd, t), lambda p: (p + start, 0, 0)),
        ],
        out_shape=[jax.ShapeDtypeStruct((t, npair * 2 * hd), bf)] + full,
        input_output_aliases={} if prev is None else {1: 1, 2: 2, 3: 3},
        compiler_params=_params(),
        cost_estimate=_cost(npair * 9.5e9, npair * 2 * t * hd * 16),
        name="attn_fwd",
    )(qkv, *([] if prev is None else prev))


def _bwd_kernel(*refs, hd, r0, r1, has_in, has_out):
    qkv_ref, tr_ref, o_ref, do_ref, lse_ref = refs[:5]
    refs = refs[5:]
    acc_in = None
    if has_in:
        acc_in, _ = refs[:2]
        refs = refs[2:]
    out_ref, full_ref = refs[:2]
    refs = refs[2:]
    acc_out = None
    if has_out:
        acc_out = refs[0]
        refs = refs[1:]
    (g_t,) = refs
    sc = hd**-0.5
    c = LOG2E * sc
    if has_in:
        g_t[...] = acc_in[0]
    for i in reversed(range(r0 // BQ, r1 // BQ)):
        w = (i + 1) * BQ
        rows = slice(i * BQ, w)
        loc = slice(i * BQ - r0, w - r0)
        blk = qkv_ref[loc, 0 : 4 * hd]
        do2 = do_ref[loc, :]
        do_t = do2.T
        lse = lse_ref[0, :, rows].T
        prod = do2.astype(f32) * o_ref[loc, :].astype(f32)
        sd = []
        for h in range(2):
            b = 3 * hd * h
            s = _dot(blk[:, b : b + hd], tr_ref[0, b + hd : b + 2 * hd, :w])
            dp = _dot(do2[:, h * hd : (h + 1) * hd], tr_ref[0, b + 2 * hd : b + 3 * hd, :w])
            sd.append((s, dp))
        ew = []
        for h in range(2):
            s, dp = sd[h]
            p = jnp.exp2(s * c - lse[:, h : h + 1])
            d = jnp.where(_causal(BQ), p[:, w - BQ :], 0.0)
            p = jnp.concatenate([p[:, : w - BQ], d], 1) if i else d
            delta = jnp.sum(prod[:, h * hd : (h + 1) * hd], axis=1, keepdims=True)
            ew.append((p.astype(bf), (p * (dp - delta)).astype(bf)))
        outs = []
        for h in range(2):
            p, ds = ew[h]
            b = 3 * hd * h
            dv = _dot(do_t[h * hd : (h + 1) * hd], p)
            dk = _dot(tr_ref[0, b : b + hd, rows], ds)
            dq = _dot_t(tr_ref[0, b + hd : b + 2 * hd, :w], ds)
            kr = slice(2 * hd * h, 2 * hd * h + hd)
            vr = slice(2 * hd * h + hd, 2 * hd * h + 2 * hd)
            if w == r1 and not has_in:
                g_t[kr, :] = dk
                g_t[vr, :] = dv
            else:
                g_t[kr, :w] += dk
                g_t[vr, :w] += dv
            outs += [(dq * sc).astype(bf), (g_t[kr, rows] * sc).astype(bf), g_t[vr, rows].astype(bf)]
        res = jnp.concatenate(outs, 0).T
        out_ref[loc, :] = res
        full_ref[loc, :] = res
    if has_out:
        acc_out[0] = g_t[:, :r0]


def _attn_bwd(qkv, tr, o, do, lse, acc, full, chunk, b, hd):
    t, w = qkv.shape
    npair = w // (6 * hd)
    r0, r1 = chunk * b, (chunk + 1) * b
    has_in, has_out = acc is not None, r0 > 0
    in_specs = [
        pl.BlockSpec((b, 6 * hd), lambda p: (chunk, p)),
        pl.BlockSpec((1, 6 * hd, r1), lambda p: (p, 0, 0)),
        pl.BlockSpec((b, 2 * hd), lambda p: (chunk, p)),
        pl.BlockSpec((b, 2 * hd), lambda p: (0, p)),
        pl.BlockSpec((1, 2, t), lambda p: (p, 0, 0)),
    ]
    args = [qkv, tr, o, do, lse]
    alias = {}
    if has_in:
        in_specs += [pl.BlockSpec((1, 4 * hd, r1), lambda p: (p, 0, 0)), pl.BlockSpec(memory_space=pl.ANY)]
        args += [acc, full]
        alias = {6: 1}
    out_specs = [pl.BlockSpec((b, 6 * hd), lambda p: (0, p)), pl.BlockSpec((b, 6 * hd), lambda p: (chunk, p))]
    out_shape = [jax.ShapeDtypeStruct((b, w), bf), jax.ShapeDtypeStruct((t, w), bf)]
    if has_out:
        out_specs.append(pl.BlockSpec((1, 4 * hd, r0), lambda p: (p, 0, 0)))
        out_shape.append(jax.ShapeDtypeStruct((npair, 4 * hd, r0), f32))
    work = npair * 2 * b * (r0 + r1)
    return pl.pallas_call(
        functools.partial(_bwd_kernel, hd=hd, r0=r0, r1=r1, has_in=has_in, has_out=has_out),
        grid=(npair,),
        in_specs=in_specs,
        out_specs=out_specs,
        out_shape=out_shape,
        scratch_shapes=[pltpu.VMEM((4 * hd, r1), f32)],
        input_output_aliases=alias,
        compiler_params=_params(),
        cost_estimate=_cost(work * 1500, 3 * t * w),
    )(*args)


def _h1_kernel(ids, x_ref, oa, ob, pa, pb, qa, qb, ra, rb, wa, wb, wc, wd, g_ref, xh_ref, rs_ref, own_ref, full_ref, acc):
    def run(first, second):
        acc[...] = sum(_dot(jnp.concatenate([u, v], 1), w[...]) for u, v, w in first + second)

    near = [(oa[0, 0], ob[0, 0], wa), (pa[0], pb[0], wb)]
    far = [(qa[0, 0], qb[0, 0], wc), (ra[0], rb[0], wd)]

    @pl.when(ids[1] == 0)
    def _():
        run(near, far)

    @pl.when(ids[1] != 0)
    def _():
        run(far, near)

    h1 = x_ref[0, 0].astype(f32) + acc[...]
    xc = h1 - jnp.mean(h1, axis=1, keepdims=True)
    rs = lax.rsqrt(jnp.mean(xc * xc, axis=1, keepdims=True) + EPS)
    xh = xc * rs
    n2 = (xh * g_ref[...].astype(f32)).astype(bf)
    xh_ref[...] = xh
    rs_ref[...] = jnp.broadcast_to(rs, (rs.shape[0], 128))
    own_ref[...] = n2
    full_ref[0] = n2


def _h1(ids, chunk, x4, o_own, o_same, o_cross, o_diag, ws, g2):
    _, _, r, d = x4.shape
    own = lambda k: pl.BlockSpec((1, 1, TILE, k), lambda i, s: (chunk, s[0], i, 0))
    row = lambda k: pl.BlockSpec((1, TILE, k), lambda i, s: (chunk, i, 0))
    flat = lambda k: pl.BlockSpec((TILE, k), lambda i, s: (i, 0))
    const = lambda shape: pl.BlockSpec(shape, lambda i, s: (0, 0), pipeline_mode=pl.Buffered(1))
    k = o_own[0].shape[-1]
    return pl.pallas_call(
        _h1_kernel,
        grid_spec=pltpu.PrefetchScalarGridSpec(
            num_scalar_prefetch=1,
            grid=(r // TILE,),
            in_specs=[own(d), own(k), own(k), row(k), row(k), own(k), own(k), row(k), row(k)]
            + [const((2 * k, d))] * 4
            + [const((1, d))],
            out_specs=[flat(d), flat(128), flat(d), pl.BlockSpec((1, TILE, d), lambda i, s: (s[0], i, 0))],
            scratch_shapes=[pltpu.VMEM((TILE, d), f32)],
        ),
        out_shape=[
            jax.ShapeDtypeStruct((r, d), f32),
            jax.ShapeDtypeStruct((r, 128), f32),
            jax.ShapeDtypeStruct((r, d), bf),
            jax.ShapeDtypeStruct((2, r, d), bf),
        ],
        compiler_params=_params(),
        cost_estimate=_cost(2 * r * d * 8 * k, 20 * MB),
    )(ids, x4, *o_own, *o_same, *o_cross, *o_diag, *ws, g2)


def _place_kernel(ids, v_ref, _, buf_ref):
    buf_ref[0] = v_ref[...]


def _place(ids, buf, v):
    r, d = v.shape
    return pl.pallas_call(
        _place_kernel,
        grid_spec=pltpu.PrefetchScalarGridSpec(
            num_scalar_prefetch=1,
            grid=(r // TILE,),
            in_specs=[pl.BlockSpec((TILE, d), lambda i, s: (i, 0)), pl.BlockSpec(memory_space=pl.ANY)],
            out_specs=pl.BlockSpec((1, TILE, d), lambda i, s: (1 - s[0], i, 0)),
        ),
        out_shape=jax.ShapeDtypeStruct(buf.shape, buf.dtype),
        input_output_aliases={2: 0},
        compiler_params=_params(32),
        cost_estimate=_cost(r * d * 1000, 2 * r * d * 2),
    )(ids, v, buf)


def _place4_kernel(ids, v_ref, _, buf_ref):
    buf_ref[0, 0] = v_ref[...]


def _place4(ids, buf, v, chunk):
    r, d = v.shape
    return pl.pallas_call(
        _place4_kernel,
        grid_spec=pltpu.PrefetchScalarGridSpec(
            num_scalar_prefetch=1,
            grid=(r // TILE,),
            in_specs=[pl.BlockSpec((TILE, d), lambda i, s: (i, 0)), pl.BlockSpec(memory_space=pl.ANY)],
            out_specs=pl.BlockSpec((1, 1, TILE, d), lambda i, s: (chunk, 1 - s[0], i, 0)),
        ),
        out_shape=jax.ShapeDtypeStruct(buf.shape, buf.dtype),
        input_output_aliases={2: 0},
        compiler_params=_params(32),
        cost_estimate=_cost(r * d * 1000, 2 * r * d * 2),
    )(ids, v, buf)


def _lnb2_kernel(ids, sa, sb, xh_ref, rs_ref, dy_ref, g_ref, dh_ref, own_ref, full_ref):
    u = (sa[...].astype(f32) + sb[...].astype(f32)) * g_ref[...].astype(f32)
    xh = xh_ref[...]
    v = u - jnp.mean(u, axis=1, keepdims=True) - xh * jnp.mean(u * xh, axis=1, keepdims=True)
    dh = dy_ref[0, 0].astype(f32) + rs_ref[:, :1] * v
    dhb = dh.astype(bf)
    dh_ref[...] = dh
    own_ref[...] = dhb
    full_ref[0] = dhb


def _lnb1_kernel(ids, sa, sb, x_ref, mu_ref, rs_ref, dh_ref, g_ref, *outs):
    u = (sa[...].astype(f32) + sb[...].astype(f32)) * g_ref[...].astype(f32)
    rs = rs_ref[0, 0].T
    xh = (x_ref[0, 0].astype(f32) - mu_ref[0, 0].T) * rs
    v = u - jnp.mean(u, axis=1, keepdims=True) - xh * jnp.mean(u * xh, axis=1, keepdims=True)
    dx = (dh_ref[...] + rs * v).astype(bf)
    outs[-2][...] = dx
    outs[-1][0, 0] = dx


def _lnb(kernel, ids, chunk, args, kinds, outs, out_kinds, alias=None, tile=128):
    r = args[0].shape[0]
    specs = {
        "flat": lambda k: pl.BlockSpec((tile, k), lambda i, s: (i, 0)),
        "own": lambda k: pl.BlockSpec((1, 1, tile, k), lambda i, s: (chunk, s[0], i, 0)),
        "stat": lambda k: pl.BlockSpec((1, 1, 1, tile), lambda i, s: (chunk, s[0], 0, i)),
        "gain": lambda k: pl.BlockSpec((1, k), lambda i, s: (0, 0)),
        "pair": lambda k: pl.BlockSpec((1, tile, k), lambda i, s: (s[0], i, 0)),
        "any": lambda k: pl.BlockSpec(memory_space=pl.ANY),
    }
    return pl.pallas_call(
        kernel,
        grid_spec=pltpu.PrefetchScalarGridSpec(
            num_scalar_prefetch=1,
            grid=(r // tile,),
            in_specs=[specs[k](a.shape[-1]) for k, a in zip(kinds, args)],
            out_specs=[specs[k](o.shape[-1]) for k, o in zip(out_kinds, outs)],
        ),
        out_shape=outs,
        input_output_aliases=alias or {},
        compiler_params=_params(32),
        cost_estimate=_cost(r * 2048 * 6000, r * 2048 * 16),
    )(ids, *args)


class _Chain:
    def __init__(self):
        self.last = None

    def tie(self, *args):
        if self.last is not None:
            *args, _ = lax.optimization_barrier((*args, self.last))
        return args if len(args) > 1 else args[0]

    def did(self, v):
        self.last = v
        return v


def solution(mesh):
    def body(x, mu1, rs1, g1, g2, dy, wqkv, wo, w1, w2):
        hl, hd, d = wo.shape
        t = x.shape[0]
        b = t // NB
        r = b // 2
        me = lax.axis_index("tp")
        core, chip = me % 2, me // 2
        ids = jnp.stack([core, chip]).astype(jnp.int32)

        def same(v):
            return lax.ppermute(v, "tp", SAME)

        def cross(v):
            return lax.ppermute(v, "tp", CROSS)

        split = lambda v: v.reshape(NB, 2, r, v.shape[-1])
        pick = lambda v, c: lax.dynamic_index_in_dim(v, c, v.ndim - 3, keepdims=False)
        sds = jax.ShapeDtypeStruct
        order = _Chain()
        tie, did = order.tie, order.did
        chunks = list(reversed(range(NB)))

        wo2 = wo.reshape(hl * hd, d)
        wo_cross = cross(wo2)
        wo_same = same(wo2)
        wo_diag = same(wo_cross)

        xf = x.astype(f32)
        n1 = ((xf - mu1[:, None]) * rs1[:, None] * g1.astype(f32)).astype(bf)
        qkv = did(_dot(n1, wqkv).astype(bf))

        o_own, o_same, o_cross, o_diag = [], [], [], []
        npair = hl // 4
        prev = None
        for s in range(2):
            o, *prev = _attn_fwd(tie(qkv), hd, s * npair, npair, prev)
            did(o)
            oc = cross(o)
            o_own.append(split(o))
            o_cross.append(split(oc))
            o_same.append(same(pick(split(o), 1 - core)))
            o_diag.append(same(pick(split(oc), 1 - core)))
        o_all, lse, qkv_t = prev

        dg = did(_dot_t(tie(dy), w2))

        x4, dy4 = split(x), split(dy)
        xh2, rs2, n2, others = [None] * NB, [None] * NB, [None] * NB, [None] * NB
        for k in chunks:
            xh2[k], rs2[k], own, n2[k] = _h1(
                ids, k, tie(x4), o_own, o_same, o_cross, o_diag, (wo2, wo_same, wo_cross, wo_diag), g2[None]
            )
            did(own)
            others[k] = same(own)

        gl, da, sums, n2f = [None] * NB, [None] * NB, [None] * NB, [None] * NB
        dyc = dy.reshape(NB, b, d)
        dgc = dg.reshape(NB, b, -1)

        def place_n2(k):
            n2f[k] = did(_place(ids, tie(n2[k]), others[k])).reshape(b, d)

        def mlp(k):
            a = _dot(tie(n2f[k]), w1)
            g, gelu_vjp = jax.vjp(jax.nn.gelu, a)
            gl[k] = g.astype(bf)
            da[k] = did(gelu_vjp(dgc[k])[0].astype(bf))

        def partial_other(v, w):
            p = did(_dot_t(pick(tie(v).reshape(2, r, -1), 1 - core), w).astype(bf))
            return same(p)

        def partial_own(v, w, recv):
            s_own = did((_dot_t(pick(tie(v).reshape(2, r, -1), core), w) + recv.astype(f32)).astype(bf))
            return s_own, cross(s_own)

        def grad(u, v, add=None, keep=False):
            p = _dot(tie(u).T, v)
            p = p if add is None else p + add
            return did(p if keep else p.astype(bf))

        place_n2(1)
        mlp(1)
        recv = partial_other(da[1], w1)
        place_n2(0)
        sums[1] = partial_own(da[1], w1, recv)
        mlp(0)
        recv = partial_other(da[0], w1)
        dw2 = grad(gl[1], dyc[1], keep=True)
        sums[0] = partial_own(da[0], w1, recv)

        dh, dhb = [None] * NB, [None] * NB

        def norm2(k):
            dh[k], own, dhb[k] = _lnb(
                _lnb2_kernel, ids, k, (tie(sums[k][0]), sums[k][1], xh2[k], rs2[k], dy4, g2[None]),
                ("flat", "flat", "flat", "flat", "own", "gain"),
                (sds((r, d), f32), sds((r, d), bf), sds((2, r, d), bf)), ("flat", "flat", "pair"),
            )
            did(own)
            return same(own)

        def attention(k, other, acc, full):
            dhb[k] = did(_place(ids, tie(dhb[k]), other)).reshape(b, d)
            do = did(_dot_t(tie(dhb[k]), wo2).astype(bf))
            res = _attn_bwd(qkv, qkv_t, o_all, do, lse, acc, full, k, b, hd)
            did(res[0])
            return res

        def norm1(k, pair, dx):
            args = (tie(pair[0]), pair[1], x4, mu4, rs4, dh[k], g1[None]) + (() if dx is None else (dx,))
            own, dx = _lnb(
                _lnb1_kernel, ids, k, args, ("flat", "flat", "own", "stat", "stat", "flat", "gain", "any")[: len(args)],
                (sds((r, d), bf), sds((NB, 2, r, d), bf)), ("flat", "own"),
                None if dx is None else {8: 1},
            )
            did(own)
            return same(own), dx

        mu4, rs4 = mu1.reshape(NB, 2, 1, r), rs1.reshape(NB, 2, 1, r)
        o3 = o_all.reshape(NB, b, -1)

        other = norm2(1)
        dw2 = grad(gl[0], dyc[0], dw2)
        dq1, full, acc = attention(1, other, None, None)
        recv = partial_other(dq1, wqkv)
        other = norm2(0)
        pair1 = partial_own(dq1, wqkv, recv)
        dq0, full = attention(0, other, acc, full)
        recv = partial_other(dq0, wqkv)
        dwo = grad(o3[1], dhb[1], keep=True)
        pair0 = partial_own(dq0, wqkv, recv)
        dwo = grad(o3[0], dhb[0], dwo).reshape(hl, hd, d)
        dw1 = grad(n2f[1], da[1], keep=True)
        dw1 = grad(n2f[0], da[0], dw1)
        other1, dx = norm1(1, pair1, None)
        dwqkv = grad(n1, full)
        other0, dx = norm1(0, pair0, dx)
        dx = _place4(ids, dx, other1, 1)
        dx = _place4(ids, dx, other0, 0)
        return dx.reshape(t, d), dwqkv, dwo, dw1, dw2

    return jax.shard_map(
        body, mesh=mesh,
        in_specs=(P("dp", None), P("dp"), P("dp"), P(None), P(None), P("dp", None),
                  P(None, "tp"), P("tp", None, None), P(None, "tp"), P("tp", None)),
        out_specs=(P("dp", None), P("dp", "tp"), P(("dp", "tp"), None, None), P("dp", "tp"), P(("dp", "tp"), None)),
        check_vma=False)
```

profile of v0, /device:TPU:0, one launch (start us, length us, event | category | flops | bytes accessed | tf_op | source)
XLA Modules:
  0.0 518.6 jit_solution(561541546315179189)
XLA Ops:
  0.6 3.3 collective-permute-start.7
  4.7 8.7 %multiply_convert_fusion = bf16[2048,2048]{1,0:T(8,128)(2,1)} fusion(bf16[2048,2048]{1,0:T(8,128)(2,1)} %param.10, f32[2048]{0:T(1024)S(1)} %convert_element_type.79, f32[2048]{0:T(1024)} %param.12, f32[2048]{0:T(1024)} %param.11), kind=kLoop, calls=%fused_computation.2 | loop fusion | flops 20971520 | bytes 16801792 | tf_op jit(solution)/shard_map/convert_element_type | solution.py:386
  13.4 16.7 %convolution_convert_fusion.refs_0_ = bf16[2048,1536]{1,0:T(8,128)(2,1)} fusion(bf16[2048,2048]{1,0:T(8,128)(2,1)} %multiply_convert_fusion, bf16[2048,1536]{1,0:T(8,128)(2,1)S(1)} %copy-done.32), kind=kOutput, calls=%fused_computation.23 | convolution fusion | flops 12888047616 | bytes 20971520 | tf_op jit(solution)/shard_map/dot_general | solution.py:24
  30.1 18.3 %attn_fwd.2 = (bf16[2048,256]{1,0:T(8,128)(2,1)}, bf16[2048,512]{1,0:T(8,128)(2,1)}, f32[4,2,2048]{2,1,0:T(2,128)}, bf16[4,384,2048]{2,1,0:T(8,128)(2,1)}) custom-call(bf16[2048,1536]{1,0:T(8,128)(2,1)} %convolution_convert_fusion.refs_0_), custom_call_target="tpu_custom_call" | custom-call | flops 19000000512 | bytes 8388608 | tf_op jit(solution)/shard_map/attn_fwd/pallas_call | solution.py:81
  48.4 19.1 %attn_fwd.3 = (bf16[2048,256]{1,0:T(8,128)(2,1)}, bf16[2048,512]{1,0:T(8,128)(2,1)}, f32[4,2,2048]{2,1,0:T(2,128)}, bf16[4,384,2048]{2,1,0:T(8,128)(2,1)}) custom-call(bf16[2048,1536]{1,0:T(8,128)(2,1)} %convolution_convert_fusion.refs_0_, bf16[2048,512]{1,0:T(8,128)(2,1)} %get-tuple-element.71.refs_1_, ...), custom_call_target="tpu_custom_call", output_to_operand_aliasing={{1}: (1, {}), {2}: (2, {}), {3}: (3, {})} | custom-call | flops 19000000512 | bytes 8388608 | tf_op jit(solution)/shard_map/attn_fwd/pallas_call | solution.py:81
  67.5 2.0 collective-permute-start.2
  71.9 21.9 %collective-permute-done.3 = bf16[2048,256]{1,0:T(8,128)(2,1)} collective-permute-done((bf16[2048,256]{1,0:T(8,128)(2,1)}, bf16[2048,256]{1,0:T(8,128)(2,1)}, u32[]{:S(2)}, u32[]{:S(2)}) %collective-permute-start.3) | collective-permute-done | bytes 1048608 | tf_op jit(solution)/shard_map/ppermute | solution.py:371
  95.7 19.2 %collective-permute-done.2 = bf16[2048,256]{1,0:T(8,128)(2,1)} collective-permute-done((bf16[2048,256]{1,0:T(8,128)(2,1)S(1)}, bf16[2048,256]{1,0:T(8,128)(2,1)}, u32[]{:S(2)}, u32[]{:S(2)}) %collective-permute-start.2) | collective-permute-done | bytes 1048608 | tf_op jit(solution)/shard_map/ppermute | solution.py:371
  117.3 24.5 %fusion.54 = f32[2048,2048]{1,0:T(8,128)} fusion(bf16[2048,2048]{1,0:T(8,128)(2,1)} %param.15, bf16[2048,2048]{1,0:T(8,128)(2,1)} %param.19), kind=kOutput, calls=%fused_computation.73 | convolution fusion | flops 17179869184 | bytes 33554432 | tf_op jit(solution)/shard_map/dot_general | solution.py:28
  144.1 13.5 %shard_map.137 = (f32[512,2048]{1,0:T(8,128)}, f32[512,128]{1,0:T(8,128)}, bf16[512,2048]{1,0:T(8,128)(2,1)}, bf16[2,512,2048]{2,1,0:T(8,128)(2,1)}) custom-call(s32[2]{0:T(128)} %pad_add_fusion.ids, bf16[2,2,512,2048]{3,2,1,0:T(8,128)(2,1)} %bitcast.97, bf16[2,2,512,256]{3,2,1,0:T(8,128)(2,1)} %bitcast.122, bf16[2,2,512,256]{3,2,1,0:T(8,128)(2,1)} %bitcast.126, ...), custom_call_target="tpu_custom_call" | custom-call | flops 4294967296 | bytes 20971520 | tf_op jit(solution)/shard_map/pallas_call | solution.py:233
  158.2 13.7 %shard_map.138 = (f32[512,2048]{1,0:T(8,128)}, f32[512,128]{1,0:T(8,128)}, bf16[512,2048]{1,0:T(8,128)(2,1)}, bf16[2,512,2048]{2,1,0:T(8,128)(2,1)}) custom-call(s32[2]{0:T(128)} %pad_add_fusion.ids, bf16[2,2,512,2048]{3,2,1,0:T(8,128)(2,1)} %bitcast.98, bf16[2,2,512,256]{3,2,1,0:T(8,128)(2,1)} %bitcast.123, bf16[2,2,512,256]{3,2,1,0:T(8,128)(2,1)} %bitcast.127, ...), custom_call_target="tpu_custom_call" | custom-call | flops 4294967296 | bytes 20971520 | tf_op jit(solution)/shard_map/pallas_call | solution.py:233
  172.0 2.2 copy-done.8
  174.2 2.4 shard_map.139
  178.6 20.0 %multiply_convert_fusion.2 = (bf16[1024,2048]{1,0:T(8,128)(2,1)}, bf16[1024,2048]{1,0:T(8,128)(2,1)S(1)}) fusion(f32[2048,2048]{1,0:T(8,128)} %fusion.54, bf16[1024,2048]{1,0:T(8,128)(2,1)} %bitcast.109, bf16[2048,2048]{1,0:T(8,128)(2,1)} %param.18), kind=kOutput, calls=%fused_computation.22 | convolution fusion | flops 8636071936 | bytes 29360128 | tf_op jit(solution)/shard_map/dot_general | solution.py:24
  198.6 5.8 %convolution_convert_fusion.5 = bf16[512,2048]{1,0:T(8,128)(2,1)} fusion(bf16[2048,2048]{1,0:T(8,128)(2,1)S(1)} %bitcast.130, bf16[2,512,2048]{2,1,0:T(8,128)(2,1)S(1)} %bitcast.135, s32[]{:T(128)S(6)} %select_n.32), kind=kOutput, calls=%fused_computation.36 | convolution fusion | flops 4296015872 | bytes 12582916 | tf_op jit(solution)/shard_map/dot_general | solution.py:28
  204.9 2.2 copy-done.4
  208.3 2.0 copy-done.5
  210.3 9.2 %add_convert_fusion.6.sa = bf16[512,2048]{1,0:T(8,128)(2,1)S(1)} fusion(bf16[512,2048]{1,0:T(8,128)(2,1)} %collective-permute-done.11, bf16[2048,2048]{1,0:T(8,128)(2,1)} %param.18, bf16[2,512,2048]{2,1,0:T(8,128)(2,1)} %bitcast.136, s32[]{:T(128)S(6)} %select_n.33), kind=kOutput, calls=%fused_computation.32 | convolution fusion | flops 4298113024 | bytes 14680068 | tf_op jit(solution)/shard_map/dot_general | solution.py:28
  219.6 17.8 %multiply_convert_fusion.1 = (bf16[1024,2048]{1,0:T(8,128)(2,1)}, bf16[1024,2048]{1,0:T(8,128)(2,1)}) fusion(f32[2048,2048]{1,0:T(8,128)} %fusion.54, bf16[1024,2048]{1,0:T(8,128)(2,1)S(1)} %bitcast.107, bf16[2048,2048]{1,0:T(8,128)(2,1)S(1)} %bitcast.132), kind=kOutput, calls=%fused_computation.21 | convolution fusion | flops 8636071936 | bytes 29360128 | tf_op jit(solution)/shard_map/dot_general | solution.py:24
  237.4 6.5 %convolution_convert_fusion.4 = bf16[512,2048]{1,0:T(8,128)(2,1)S(1)} fusion(bf16[2048,2048]{1,0:T(8,128)(2,1)S(1)} %bitcast.132, bf16[2,512,2048]{2,1,0:T(8,128)(2,1)} %bitcast.137, s32[]{:T(128)S(6)} %select_n.32), kind=kOutput, calls=%fused_computation.35 | convolution fusion | flops 4296015872 | bytes 12582916 | tf_op jit(solution)/shard_map/dot_general | solution.py:28
  244.2 14.4 %fusion.15 = f32[2048,2048]{1,0:T(8,128)} fusion(bf16[1024,2048]{1,0:T(8,128)(2,1)S(1)} %copy-done.36, bf16[2048,2048]{1,0:T(8,128)(2,1)} %param.15), kind=kOutput, calls=%fused_computation.30 | convolution fusion | flops 8589934592 | bytes 25165824 | tf_op jit(solution)/shard_map/dot_general | solution.py:24
  258.7 8.7 %add_convert_fusion.5.sa = bf16[512,2048]{1,0:T(8,128)(2,1)S(1)} fusion(bf16[512,2048]{1,0:T(8,128)(2,1)S(1)} %collective-permute-done.12, bf16[2048,2048]{1,0:T(8,128)(2,1)} %param.18, bf16[2,512,2048]{2,1,0:T(8,128)(2,1)} %bitcast.138, s32[]{:T(128)S(6)} %select_n.33), kind=kOutput, calls=%fused_computation.29 | convolution fusion | flops 4298113024 | bytes 14680068 | tf_op jit(solution)/shard_map/dot_general | solution.py:28
  269.1 23.3 %collective-permute-done.13.sb = bf16[512,2048]{1,0:T(8,128)(2,1)S(1)} collective-permute-done((bf16[512,2048]{1,0:T(8,128)(2,1)S(1)}, bf16[512,2048]{1,0:T(8,128)(2,1)S(1)}, u32[]{:S(2)}, u32[]{:S(2)}) %collective-permute-start.13) | collective-permute-done | bytes 2097184 | tf_op jit(solution)/shard_map/ppermute | solution.py:371
  292.4 5.6 %shard_map.141 = (f32[512,2048]{1,0:T(8,128)S(1)}, bf16[512,2048]{1,0:T(8,128)(2,1)}, bf16[2,512,2048]{2,1,0:T(8,128)(2,1)S(1)}) custom-call(s32[2]{0:T(128)S(1)} %copy-done.14, bf16[512,2048]{1,0:T(8,128)(2,1)S(1)} %add_convert_fusion.6.sa, bf16[512,2048]{1,0:T(8,128)(2,1)S(1)} %collective-permute-done.13.sb, f32[512,2048]{1,0:T(8,128)S(1)} %copy-done.18, ...), custom_call_target="tpu_custom_call" | custom-call | flops 6291456000 | bytes 16777216 | tf_op jit(solution)/shard_map/pallas_call | solution.py:328
  298.0 1.9 copy-done.21
  300.0 16.7 %add_convert_fusion.1 = bf16[2048,2048]{1,0:T(8,128)(2,1)} fusion(f32[2048,2048]{1,0:T(8,128)} %fusion.15, bf16[1024,2048]{1,0:T(8,128)(2,1)} %get-tuple-element.98, bf16[2048,2048]{1,0:T(8,128)(2,1)} %param.15), kind=kOutput, calls=%fused_computation.1 | convolution fusion | flops 8598323200 | bytes 33554432 | tf_op jit(solution)/shard_map/dot_general | solution.py:24
  318.2 3.4 convolution_convert_fusion.7.refs_3_
  321.6 38.4 %shard_map.143 = (bf16[1024,1536]{1,0:T(8,128)(2,1)}, bf16[2048,1536]{1,0:T(8,128)(2,1)}, f32[4,256,1024]{2,1,0:T(8,128)}) custom-call(bf16[2048,1536]{1,0:T(8,128)(2,1)} %convolution_convert_fusion.refs_0_, bf16[4,384,2048]{2,1,0:T(8,128)(2,1)} %get-tuple-element.74.refs_1_, bf16[2048,512]{1,0:T(8,128)(2,1)} %get-tuple-element.75.refs_2_, ...), custom_call_target="tpu_custom_call" | custom-call | flops 37748736000 | bytes 9437184 | tf_op jit(solution)/shard_map/pallas_call | solution.py:187
  360.1 6.9 %convolution_convert_fusion.3 = bf16[512,2048]{1,0:T(8,128)(2,1)S(1)} fusion(bf16[2048,1536]{1,0:T(8,128)(2,1)} %param.16, bf16[2,512,1536]{2,1,0:T(8,128)(2,1)} %bitcast.141, s32[]{:T(128)S(6)} %select_n.32), kind=kOutput, calls=%fused_computation.34 | convolution fusion | flops 3222274048 | bytes 9961476 | tf_op jit(solution)/shard_map/dot_general | solution.py:28
  367.5 5.2 %shard_map.144 = (f32[512,2048]{1,0:T(8,128)S(1)}, bf16[512,2048]{1,0:T(8,128)(2,1)S(1)}, bf16[2,512,2048]{2,1,0:T(8,128)(2,1)S(1)}) custom-call(s32[2]{0:T(128)S(1)} %copy-done.14, bf16[512,2048]{1,0:T(8,128)(2,1)S(1)} %add_convert_fusion.5.sa, bf16[512,2048]{1,0:T(8,128)(2,1)} %collective-permute-done.15.sb, f32[512,2048]{1,0:T(8,128)S(1)} %copy-done.17, ...), custom_call_target="tpu_custom_call" | custom-call | flops 6291456000 | bytes 16777216 | tf_op jit(solution)/shard_map/pallas_call | solution.py:328
  372.7 9.5 %add_convert_fusion.4.sa = bf16[512,2048]{1,0:T(8,128)(2,1)} fusion(bf16[512,2048]{1,0:T(8,128)(2,1)S(1)} %collective-permute-done.17, bf16[2048,1536]{1,0:T(8,128)(2,1)} %param.16, bf16[2,512,1536]{2,1,0:T(8,128)(2,1)} %bitcast.142, s32[]{:T(128)S(6)} %select_n.33), kind=kOutput, calls=%fused_computation.27 | convolution fusion | flops 3224371200 | bytes 12058628 | tf_op jit(solution)/shard_map/dot_general | solution.py:28
  383.8 3.4 convolution_convert_fusion.6.refs_3_
  387.2 18.2 %shard_map.146 = (bf16[1024,1536]{1,0:T(8,128)(2,1)}, bf16[2048,1536]{1,0:T(8,128)(2,1)}) custom-call(bf16[2048,1536]{1,0:T(8,128)(2,1)} %convolution_convert_fusion.refs_0_, bf16[4,384,2048]{2,1,0:T(8,128)(2,1)} %get-tuple-element.74.refs_1_, bf16[2048,512]{1,0:T(8,128)(2,1)} %get-tuple-element.75.refs_2_, ...), custom_call_target="tpu_custom_call", output_to_operand_aliasing={{1}: (6, {})} | custom-call | flops 12582912000 | bytes 9437184 | tf_op jit(solution)/shard_map/pallas_call | solution.py:187
  405.4 6.9 %convolution_convert_fusion.2 = bf16[512,2048]{1,0:T(8,128)(2,1)S(1)} fusion(bf16[2048,1536]{1,0:T(8,128)(2,1)} %param.16, bf16[2,512,1536]{2,1,0:T(8,128)(2,1)} %bitcast.139, s32[]{:T(128)S(6)} %select_n.32), kind=kOutput, calls=%fused_computation.33 | convolution fusion | flops 3222274048 | bytes 9961476 | tf_op jit(solution)/shard_map/dot_general | solution.py:28
  414.4 2.4 fusion.55
  416.9 7.8 %add_convert_fusion.3.sa = bf16[512,2048]{1,0:T(8,128)(2,1)} fusion(bf16[512,2048]{1,0:T(8,128)(2,1)S(1)} %collective-permute-done.18, bf16[2048,1536]{1,0:T(8,128)(2,1)} %param.16, bf16[2,512,1536]{2,1,0:T(8,128)(2,1)S(1)} %bitcast.140, s32[]{:T(128)S(6)} %select_n.33), kind=kOutput, calls=%fused_computation.26 | convolution fusion | flops 3224371200 | bytes 12058628 | tf_op jit(solution)/shard_map/dot_general | solution.py:28
  425.0 3.7 add_convert_fusion.2
  428.7 11.8 %fusion.56 = f32[2048,2048]{1,0:T(8,128)} fusion(bf16[1024,2048]{1,0:T(8,128)(2,1)S(1)} %bitcast.110, bf16[1024,2048]{1,0:T(8,128)(2,1)S(1)} %copy-done.34), kind=kOutput, calls=%fused_computation.75 | convolution fusion | flops 8589934592 | bytes 25165824 | tf_op jit(solution)/shard_map/dot_general | solution.py:24
  440.5 15.9 %add_convert_fusion = bf16[2048,2048]{1,0:T(8,128)(2,1)} fusion(f32[2048,2048]{1,0:T(8,128)} %fusion.56, bf16[1024,2048]{1,0:T(8,128)(2,1)S(1)} %bitcast.108, bf16[1024,2048]{1,0:T(8,128)(2,1)} %get-tuple-element.92), kind=kOutput, calls=%fused_computation | convolution fusion | flops 8598323200 | bytes 33554432 | tf_op jit(solution)/shard_map/dot_general | solution.py:24
  456.5 4.9 collective-permute-done.19.sb
  461.4 2.2 copy-done.22
  463.5 6.3 %shard_map.147 = (bf16[512,2048]{1,0:T(8,128)(2,1)S(1)}, bf16[2,2,512,2048]{3,2,1,0:T(8,128)(2,1)}) custom-call(s32[2]{0:T(128)S(1)} %copy-done.14, bf16[512,2048]{1,0:T(8,128)(2,1)} %add_convert_fusion.4.sa, bf16[512,2048]{1,0:T(8,128)(2,1)} %collective-permute-done.19.sb, bf16[2,2,512,2048]{3,2,1,0:T(8,128)(2,1)S(1)} %bitcast.101, ...), custom_call_target="tpu_custom_call" | custom-call | flops 6291456000 | bytes 16777216 | tf_op jit(solution)/shard_map/pallas_call | solution.py:328
  469.8 19.5 %convolution_convert_fusion.1 = bf16[2048,1536]{1,0:T(8,128)(2,1)} fusion(bf16[2048,2048]{1,0:T(8,128)(2,1)} %multiply_convert_fusion, bf16[2048,1536]{1,0:T(8,128)(2,1)} %get-tuple-element.125), kind=kOutput, calls=%fused_computation.24 | convolution fusion | flops 12888047616 | bytes 20971520 | tf_op jit(solution)/shard_map/dot_general | solution.py:24
  489.3 16.4 %collective-permute-done.20.sb = bf16[512,2048]{1,0:T(8,128)(2,1)} collective-permute-done((bf16[512,2048]{1,0:T(8,128)(2,1)}, bf16[512,2048]{1,0:T(8,128)(2,1)}, u32[]{:S(2)}, u32[]{:S(2)}) %collective-permute-start.20) | collective-permute-done | bytes 2097184 | tf_op jit(solution)/shard_map/ppermute | solution.py:371
  505.8 6.3 %shard_map.148 = (bf16[512,2048]{1,0:T(8,128)(2,1)S(1)}, bf16[2,2,512,2048]{3,2,1,0:T(8,128)(2,1)}) custom-call(s32[2]{0:T(128)S(1)} %copy-done.14, bf16[512,2048]{1,0:T(8,128)(2,1)} %add_convert_fusion.3.sa, bf16[512,2048]{1,0:T(8,128)(2,1)} %collective-permute-done.20.sb, bf16[2,2,512,2048]{3,2,1,0:T(8,128)(2,1)S(1)} %bitcast.102, ...), custom_call_target="tpu_custom_call", output_to_operand_aliasing={{1}: (8, {})} | custom-call | flops 6291456000 | bytes 16777216 | tf_op jit(solution)/shard_map/pallas_call | solution.py:328
  512.1 2.0 shard_map.149._
  514.1 2.2 collective-permute-done.21.v_ref
  516.3 1.9 shard_map.150
  (134 shorter events, 22.3 us)
Async XLA Ops:
  0.6 116.6 %collective-permute-start.7 = (bf16[512,2048]{1,0:T(8,128)(2,1)}, bf16[512,2048]{1,0:T(8,128)(2,1)}, u32[]{:S(2)}, u32[]{:S(2)}) collective-permute-start(bf16[512,2048]{1,0:T(8,128)(2,1)} %bitcast.116), channel_id=1, source_target_pairs={{0,2},{2,0},{1,3},{3,1},{4,6},{6,4},{5,7},{7,5}} | collective-permute-start | bytes 6291464 | tf_op jit(solution)/shard_map/ppermute | solution.py:371
  4.6 8.7 %copy-start.32 = (bf16[2048,1536]{1,0:T(8,128)(2,1)S(1)}, bf16[2048,1536]{1,0:T(8,128)(2,1)}, u32[]{:S(2)}) copy-start(bf16[2048,1536]{1,0:T(8,128)(2,1)} %param.16) | copy-start | bytes 18874372
  48.3 19.1 %copy-start.26 = (bf16[2048,256]{1,0:T(8,128)(2,1)S(1)}, bf16[2048,256]{1,0:T(8,128)(2,1)}, u32[]{:S(2)}) copy-start(bf16[2048,256]{1,0:T(8,128)(2,1)} %get-tuple-element.69) | copy-start | bytes 3145732
  48.4 22.3 %copy-start.23 = (bf16[8,64,2048]{2,1,0:T(8,128)(2,1)S(1)}, bf16[8,64,2048]{2,1,0:T(8,128)(2,1)}, u32[]{:S(2)}) copy-start(bf16[8,64,2048]{2,1,0:T(8,128)(2,1)} %param.17) | copy-start | bytes 6291460
  67.5 26.3 %collective-permute-start.3 = (bf16[2048,256]{1,0:T(8,128)(2,1)}, bf16[2048,256]{1,0:T(8,128)(2,1)}, u32[]{:S(2)}, u32[]{:S(2)}) collective-permute-start(bf16[2048,256]{1,0:T(8,128)(2,1)} %get-tuple-element.76), channel_id=1, source_target_pairs={{0,2},{2,0},{1,3},{3,1},{4,6},{6,4},{5,7},{7,5}} | collective-permute-start | bytes 3145736 | tf_op jit(solution)/shard_map/ppermute | solution.py:371
  67.5 47.4 %collective-permute-start.2 = (bf16[2048,256]{1,0:T(8,128)(2,1)S(1)}, bf16[2048,256]{1,0:T(8,128)(2,1)}, u32[]{:S(2)}, u32[]{:S(2)}) collective-permute-start(bf16[2048,256]{1,0:T(8,128)(2,1)S(1)} %copy-done.26), channel_id=1, source_target_pairs={{0,2},{2,0},{1,3},{3,1},{4,6},{6,4},{5,7},{7,5}} | collective-permute-start | bytes 3145736 | tf_op jit(solution)/shard_map/ppermute | solution.py:371
  70.6 46.2 %collective-permute-start.1 = (bf16[2,512,256]{2,1,0:T(8,128)(2,1)S(1)}, bf16[2,512,256]{2,1,0:T(8,128)(2,1)}, u32[]{:S(2)}, u32[]{:S(2)}) collective-permute-start(bf16[2,512,256]{2,1,0:T(8,128)(2,1)S(1)} %dynamic-slice_bitcast_fusion.2), channel_id=1, source_target_pairs={{0,1},{1,0},{2,3},{3,2},{4,5},{5,4},{6,7},{7,6}} | collective-permute-start | bytes 1572872 | tf_op jit(solution)/shard_map/ppermute | solution.py:368
  70.6 72.5 %collective-permute-start.6 = (bf16[512,2048]{1,0:T(8,128)(2,1)S(1)}, bf16[512,2048]{1,0:T(8,128)(2,1)}, u32[]{:S(2)}, u32[]{:S(2)}) collective-permute-start(bf16[512,2048]{1,0:T(8,128)(2,1)S(1)} %bitcast.119), channel_id=1, source_target_pairs={{0,1},{1,0},{2,3},{3,2},{4,5},{5,4},{6,7},{7,6}} | collective-permute-start | bytes 6291464 | tf_op jit(solution)/shard_map/ppermute | solution.py:368
  93.8 49.3 %collective-permute-start = (bf16[2,512,256]{2,1,0:T(8,128)(2,1)}, bf16[2,512,256]{2,1,0:T(8,128)(2,1)}, u32[]{:S(2)}, u32[]{:S(2)}) collective-permute-start(bf16[2,512,256]{2,1,0:T(8,128)(2,1)} %dynamic-slice_bitcast_fusion.3), channel_id=1, source_target_pairs={{0,1},{1,0},{2,3},{3,2},{4,5},{5,4},{6,7},{7,6}} | collective-permute-start | bytes 1572872 | tf_op jit(solution)/shard_map/ppermute | solution.py:368
  114.9 28.2 %collective-permute-start.5 = (bf16[2,512,256]{2,1,0:T(8,128)(2,1)}, bf16[2,512,256]{2,1,0:T(8,128)(2,1)S(1)}, u32[]{:S(2)}, u32[]{:S(2)}) collective-permute-start(bf16[2,512,256]{2,1,0:T(8,128)(2,1)} %dynamic-slice_bitcast_fusion), channel_id=1, source_target_pairs={{0,1},{1,0},{2,3},{3,2},{4,5},{5,4},{6,7},{7,6}} | collective-permute-start | bytes 1572872 | tf_op jit(solution)/shard_map/ppermute | solution.py:368
  116.7 25.1 %copy-start.31 = (bf16[2048]{0:T(1024)(128)(2,1)S(1)}, bf16[2048]{0:T(1024)(128)(2,1)}, u32[]{:S(2)}) copy-start(bf16[2048]{0:T(1024)(128)(2,1)} %param.14) | copy-start | bytes 12292
  116.7 26.3 %collective-permute-start.4 = (bf16[2,512,256]{2,1,0:T(8,128)(2,1)}, bf16[2,512,256]{2,1,0:T(8,128)(2,1)S(1)}, u32[]{:S(2)}, u32[]{:S(2)}) collective-permute-start(bf16[2,512,256]{2,1,0:T(8,128)(2,1)} %dynamic-slice_bitcast_fusion.1), channel_id=1, source_target_pairs={{0,1},{1,0},{2,3},{3,2},{4,5},{5,4},{6,7},{7,6}} | collective-permute-start | bytes 1572872 | tf_op jit(solution)/shard_map/ppermute | solution.py:368
  117.3 25.9 %collective-permute-start.8 = (bf16[512,2048]{1,0:T(8,128)(2,1)}, bf16[512,2048]{1,0:T(8,128)(2,1)}, u32[]{:S(2)}, u32[]{:S(2)}) collective-permute-start(bf16[512,2048]{1,0:T(8,128)(2,1)} %collective-permute-done.7.wc), channel_id=1, source_target_pairs={{0,1},{1,0},{2,3},{3,2},{4,5},{5,4},{6,7},{7,6}} | collective-permute-start | bytes 6291464 | tf_op jit(solution)/shard_map/ppermute | solution.py:368
  157.6 14.4 %copy-start.14 = (s32[2]{0:T(128)S(1)}, s32[2]{0:T(128)}, u32[]{:S(2)}) copy-start(s32[2]{0:T(128)} %pad_add_fusion.ids) | copy-start | bytes 28
  157.6 14.4 %collective-permute-start.10 = (bf16[512,2048]{1,0:T(8,128)(2,1)}, bf16[512,2048]{1,0:T(8,128)(2,1)}, u32[]{:S(2)}, u32[]{:S(2)}) collective-permute-start(bf16[512,2048]{1,0:T(8,128)(2,1)} %get-tuple-element.79), channel_id=1, source_target_pairs={{0,1},{1,0},{2,3},{3,2},{4,5},{5,4},{6,7},{7,6}} | collective-permute-start | bytes 6291464 | tf_op jit(solution)/shard_map/ppermute | solution.py:368
  171.9 33.0 %collective-permute-start.9 = (bf16[512,2048]{1,0:T(8,128)(2,1)}, bf16[512,2048]{1,0:T(8,128)(2,1)S(1)}, u32[]{:S(2)}, u32[]{:S(2)}) collective-permute-start(bf16[512,2048]{1,0:T(8,128)(2,1)} %get-tuple-element.81), channel_id=1, source_target_pairs={{0,1},{1,0},{2,3},{3,2},{4,5},{5,4},{6,7},{7,6}} | collective-permute-start | bytes 6291464 | tf_op jit(solution)/shard_map/ppermute | solution.py:368
  174.2 24.4 %slice-start.2 = ((s8[8388608]{0:T(1024)(128)(4,1)}), s8[4194304]{0:T(1024)(128)(4,1)S(1)}, s32[]{:S(2)}) async-start(s8[8388608]{0:T(1024)(128)(4,1)} %bitcast.129), calls=%async_computation.2 | async-start | bytes 8388608
  178.6 20.0 %slice-start.3 = ((s8[8388608]{0:T(1024)(128)(4,1)}), s8[4194304]{0:T(1024)(128)(4,1)S(1)}, s32[]{:S(2)}) async-start(s8[8388608]{0:T(1024)(128)(4,1)} %bitcast.129), calls=%async_computation.3 | async-start | bytes 8388608
  204.5 5.8 %collective-permute-start.11 = (bf16[512,2048]{1,0:T(8,128)(2,1)}, bf16[512,2048]{1,0:T(8,128)(2,1)}, u32[]{:S(2)}, u32[]{:S(2)}) collective-permute-start(bf16[512,2048]{1,0:T(8,128)(2,1)} %convolution_convert_fusion.5), channel_id=1, source_target_pairs={{0,1},{1,0},{2,3},{3,2},{4,5},{5,4},{6,7},{7,6}} | collective-permute-start | bytes 6291464 | tf_op jit(solution)/shard_map/ppermute | solution.py:368
  207.1 12.4 %slice-start.4 = ((s8[8388608]{0:T(1024)(128)(4,1)}), s8[4194304]{0:T(1024)(128)(4,1)S(1)}, s32[]{:S(2)}) async-start(s8[8388608]{0:T(1024)(128)(4,1)} %bitcast.131), calls=%async_computation.4 | async-start | bytes 8388608
  210.3 9.3 %copy-start.6 = (bf16[2,512,2048]{2,1,0:T(8,128)(2,1)S(1)}, bf16[2,512,2048]{2,1,0:T(8,128)(2,1)}, u32[]{:S(2)}) copy-start(bf16[2,512,2048]{2,1,0:T(8,128)(2,1)} %copy-done.5) | copy-start | bytes 12582916
  210.3 9.3 %slice-start.5 = ((s8[8388608]{0:T(1024)(128)(4,1)}), s8[4194304]{0:T(1024)(128)(4,1)S(1)}, s32[]{:S(2)}) async-start(s8[8388608]{0:T(1024)(128)(4,1)} %bitcast.131), calls=%async_computation.5 | async-start | bytes 8388608
  243.9 14.8 %collective-permute-start.12 = (bf16[512,2048]{1,0:T(8,128)(2,1)S(1)}, bf16[512,2048]{1,0:T(8,128)(2,1)S(1)}, u32[]{:S(2)}, u32[]{:S(2)}) collective-permute-start(bf16[512,2048]{1,0:T(8,128)(2,1)S(1)} %convolution_convert_fusion.4), channel_id=1, source_target_pairs={{0,1},{1,0},{2,3},{3,2},{4,5},{5,4},{6,7},{7,6}} | collective-permute-start | bytes 6291464 | tf_op jit(solution)/shard_map/ppermute | solution.py:368
  243.9 48.5 %collective-permute-start.13 = (bf16[512,2048]{1,0:T(8,128)(2,1)S(1)}, bf16[512,2048]{1,0:T(8,128)(2,1)S(1)}, u32[]{:S(2)}, u32[]{:S(2)}) collective-permute-start(bf16[512,2048]{1,0:T(8,128)(2,1)S(1)} %add_convert_fusion.6.sa), channel_id=1, source_target_pairs={{0,2},{2,0},{1,3},{3,1},{4,6},{6,4},{5,7},{7,5}} | collective-permute-start | bytes 6291464 | tf_op jit(solution)/shard_map/ppermute | solution.py:371
  258.7 33.8 %copy-start.13 = (bf16[1,2048]{1,0:T(2,128)(2,1)S(1)}, bf16[1,2048]{1,0:T(2,128)(2,1)}, u32[]{:S(2)}) copy-start(bf16[1,2048]{1,0:T(2,128)(2,1)} %broadcast_in_dim.4.g_ref) | copy-start | bytes 12292
  258.7 33.8 %copy-start.18 = (f32[512,2048]{1,0:T(8,128)S(1)}, f32[512,2048]{1,0:T(8,128)}, u32[]{:S(2)}) copy-start(f32[512,2048]{1,0:T(8,128)} %get-tuple-element.94.xh_ref) | copy-start | bytes 12582916
  258.7 33.8 %copy-start.20 = (f32[512,128]{1,0:T(8,128)S(1)}, f32[512,128]{1,0:T(8,128)}, u32[]{:S(2)}) copy-start(f32[512,128]{1,0:T(8,128)} %get-tuple-element.95.rs_ref) | copy-start | bytes 786436
  267.4 100.1 %collective-permute-start.15 = (bf16[512,2048]{1,0:T(8,128)(2,1)S(1)}, bf16[512,2048]{1,0:T(8,128)(2,1)}, u32[]{:S(2)}, u32[]{:S(2)}) collective-permute-start(bf16[512,2048]{1,0:T(8,128)(2,1)S(1)} %add_convert_fusion.5.sa), channel_id=1, source_target_pairs={{0,2},{2,0},{1,3},{3,1},{4,6},{6,4},{5,7},{7,5}} | collective-permute-start | bytes 6291464 | tf_op jit(solution)/shard_map/ppermute | solution.py:371
  300.0 16.7 %collective-permute-start.14 = (bf16[512,2048]{1,0:T(8,128)(2,1)}, bf16[512,2048]{1,0:T(8,128)(2,1)S(1)}, u32[]{:S(2)}, u32[]{:S(2)}) collective-permute-start(bf16[512,2048]{1,0:T(8,128)(2,1)} %get-tuple-element.96), channel_id=1, source_target_pairs={{0,1},{1,0},{2,3},{3,2},{4,5},{5,4},{6,7},{7,6}} | collective-permute-start | bytes 6291464 | tf_op jit(solution)/shard_map/ppermute | solution.py:368
  360.0 7.4 %copy-start.17 = (f32[512,2048]{1,0:T(8,128)S(1)}, f32[512,2048]{1,0:T(8,128)}, u32[]{:S(2)}) copy-start(f32[512,2048]{1,0:T(8,128)} %get-tuple-element.105.xh_ref) | copy-start | bytes 12582916
  360.0 7.4 %copy-start.19 = (f32[512,128]{1,0:T(8,128)S(1)}, f32[512,128]{1,0:T(8,128)}, u32[]{:S(2)}) copy-start(f32[512,128]{1,0:T(8,128)} %get-tuple-element.106.rs_ref) | copy-start | bytes 786436
  366.9 5.8 %collective-permute-start.17 = (bf16[512,2048]{1,0:T(8,128)(2,1)S(1)}, bf16[512,2048]{1,0:T(8,128)(2,1)S(1)}, u32[]{:S(2)}, u32[]{:S(2)}) collective-permute-start(bf16[512,2048]{1,0:T(8,128)(2,1)S(1)} %convolution_convert_fusion.3), channel_id=1, source_target_pairs={{0,1},{1,0},{2,3},{3,2},{4,5},{5,4},{6,7},{7,6}} | collective-permute-start | bytes 6291464 | tf_op jit(solution)/shard_map/ppermute | solution.py:368
  372.7 9.6 %copy-start.11 = (f32[512,2048]{1,0:T(8,128)}, f32[512,2048]{1,0:T(8,128)S(1)}, u32[]{:S(2)}) copy-start(f32[512,2048]{1,0:T(8,128)S(1)} %get-tuple-element.127.dh_ref) | copy-start | bytes 12582916
  372.7 9.6 %collective-permute-start.16 = (bf16[512,2048]{1,0:T(8,128)(2,1)S(1)}, bf16[512,2048]{1,0:T(8,128)(2,1)S(1)}, u32[]{:S(2)}, u32[]{:S(2)}) collective-permute-start(bf16[512,2048]{1,0:T(8,128)(2,1)S(1)} %get-tuple-element.107), channel_id=1, source_target_pairs={{0,1},{1,0},{2,3},{3,2},{4,5},{5,4},{6,7},{7,6}} | collective-permute-start | bytes 6291464 | tf_op jit(solution)/shard_map/ppermute | solution.py:368
  405.4 6.9 %copy-start.30 = (bf16[2048]{0:T(1024)(128)(2,1)S(1)}, bf16[2048]{0:T(1024)(128)(2,1)}, u32[]{:S(2)}) copy-start(bf16[2048]{0:T(1024)(128)(2,1)} %param.13) | copy-start | bytes 12292
  405.4 6.9 %copy-start.29 = (bf16[2048,512]{1,0:T(8,128)(2,1)S(1)}, bf16[2048,512]{1,0:T(8,128)(2,1)}, u32[]{:S(2)}) copy-start(bf16[2048,512]{1,0:T(8,128)(2,1)} %get-tuple-element.75.refs_2_) | copy-start | bytes 6291460
  412.3 4.6 collective-permute-start.18
  412.5 48.8 %collective-permute-start.19 = (bf16[512,2048]{1,0:T(8,128)(2,1)}, bf16[512,2048]{1,0:T(8,128)(2,1)}, u32[]{:S(2)}, u32[]{:S(2)}) collective-permute-start(bf16[512,2048]{1,0:T(8,128)(2,1)} %add_convert_fusion.4.sa), channel_id=1, source_target_pairs={{0,2},{2,0},{1,3},{3,1},{4,6},{6,4},{5,7},{7,5}} | collective-permute-start | bytes 6291464 | tf_op jit(solution)/shard_map/ppermute | solution.py:371
  416.9 8.1 %copy-start.3 = (bf16[2,512,2048]{2,1,0:T(8,128)(2,1)S(1)}, bf16[2,512,2048]{2,1,0:T(8,128)(2,1)}, u32[]{:S(2)}) copy-start(bf16[2,512,2048]{2,1,0:T(8,128)(2,1)} %copy-done.2) | copy-start | bytes 12582916
  424.7 81.1 %collective-permute-start.20 = (bf16[512,2048]{1,0:T(8,128)(2,1)}, bf16[512,2048]{1,0:T(8,128)(2,1)}, u32[]{:S(2)}, u32[]{:S(2)}) collective-permute-start(bf16[512,2048]{1,0:T(8,128)(2,1)} %add_convert_fusion.3.sa), channel_id=1, source_target_pairs={{0,2},{2,0},{1,3},{3,1},{4,6},{6,4},{5,7},{7,5}} | collective-permute-start | bytes 6291464 | tf_op jit(solution)/shard_map/ppermute | solution.py:371
  428.7 11.8 %copy-start.7 = (bf16[2,512,2048]{2,1,0:T(8,128)(2,1)S(1)}, bf16[2,512,2048]{2,1,0:T(8,128)(2,1)}, u32[]{:S(2)}) copy-start(bf16[2,512,2048]{2,1,0:T(8,128)(2,1)} %copy-done.5) | copy-start | bytes 12582916
  428.7 32.6 %slice-start = ((s8[8388608]{0:T(1024)(128)(4,1)}), s8[4194304]{0:T(1024)(128)(4,1)S(1)}, s32[]{:S(2)}) async-start(s8[8388608]{0:T(1024)(128)(4,1)} %bitcast.99), calls=%async_computation | async-start | bytes 8388608
  440.5 20.8 %slice-start.1 = ((s8[8388608]{0:T(1024)(128)(4,1)}), s8[4194304]{0:T(1024)(128)(4,1)S(1)}, s32[]{:S(2)}) async-start(s8[8388608]{0:T(1024)(128)(4,1)} %bitcast.99), calls=%async_computation.1 | async-start | bytes 8388608
  440.5 20.8 %copy-start.15 = (f32[2048]{0:T(1024)S(1)}, f32[2048]{0:T(1024)}, u32[]{:S(2)}) copy-start(f32[2048]{0:T(1024)} %param.12) | copy-start | bytes 24580
  440.5 20.8 %copy-start.16 = (f32[2048]{0:T(1024)S(1)}, f32[2048]{0:T(1024)}, u32[]{:S(2)}) copy-start(f32[2048]{0:T(1024)} %param.11) | copy-start | bytes 24580
  469.8 42.3 %collective-permute-start.22 = (bf16[512,2048]{1,0:T(8,128)(2,1)S(1)}, bf16[512,2048]{1,0:T(8,128)(2,1)S(1)}, u32[]{:S(2)}, u32[]{:S(2)}) collective-permute-start(bf16[512,2048]{1,0:T(8,128)(2,1)S(1)} %get-tuple-element.123), channel_id=1, source_target_pairs={{0,1},{1,0},{2,3},{3,2},{4,5},{5,4},{6,7},{7,6}} | collective-permute-start | bytes 6291464 | tf_op jit(solution)/shard_map/ppermute | solution.py:368
  469.8 35.9 %copy-start.12 = (f32[512,2048]{1,0:T(8,128)S(1)}, f32[512,2048]{1,0:T(8,128)}, u32[]{:S(2)}) copy-start(f32[512,2048]{1,0:T(8,128)} %copy-done.11) | copy-start | bytes 12582916
  512.1 4.2 collective-permute-start.21
  (18 other events, 50.7 us)
where the time goes:
time: 527 us; the launch traced here: 519 us
  matrix products  231 us (44%)
  Pallas kernels  154 us (29%)
  waiting for transfers between devices  87.9 us (17%)
  local copies, waits for them, and re-layouts  23.2 us (4%)
  starting transfers between devices  10.9 us (2%)
  other arithmetic  10.1 us (2%)
    dot_general x10, matrix products, _dot(): return jnp.dot(a, b, preferred_element_type=f32)  139 us
    dot_general x11, matrix products, _dot_t(): lax.dot_general(a, b, (((1,), (1,)), ((), ())), preferred_element_type=f32)  92.6 us
    ppermute x7, waiting for transfers between devices, cross(): return lax.ppermute(v, 'tp', CROSS)  85.7 us
    pallas_call x2, Pallas kernels, _attn_bwd(): pl.pallas_call(functools.partial(_bwd_kernel, hd=hd, r0=r0, r1=r1, has_in...  56.6 us
    pallas_call x2, Pallas kernels, _attn_fwd(): pl.pallas_call(functools.partial(_fwd_kernel, t=t, hd=hd, first=prev is N...  37.4 us
    pallas_call x2, Pallas kernels, _h1(): pl.pallas_call(_h1_kernel, grid_spec=pltpu.PrefetchScalarGridSpec(num_sca...  27.3 us
    pallas_call x4, Pallas kernels, _lnb(): pl.pallas_call(kernel, grid_spec=pltpu.PrefetchScalarGridSpec(num_scalar_...  23.4 us
    unnamed x86, local copies, waits for them, and re-layouts  16.8 us
  transfers between devices with their start and end apart: 23, of which 6 were waited for; matrix products, arithmetic and copies ran while one was open for 39% of the time, Pallas kernels for 23%

commit v1 on v0

--- a/solution.py
+++ b/solution.py
@@ -97,14 +97,14 @@
 
 
 def _bwd_kernel(*refs, hd, r0, r1, has_in, has_out):
-    qkv_ref, tr_ref, o_ref, do_ref, lse_ref = refs[:5]
-    refs = refs[5:]
+    ids, qkv_ref, tr_ref, o_ref, do_ref, lse_ref = refs[:6]
+    refs = refs[6:]
     acc_in = None
     if has_in:
         acc_in, _ = refs[:2]
         refs = refs[2:]
-    out_ref, full_ref = refs[:2]
-    refs = refs[2:]
+    own_ref, other_ref, full_ref = refs[:3]
+    refs = refs[3:]
     acc_out = None
     if has_out:
         acc_out = refs[0]
@@ -153,56 +153,60 @@
                 g_t[kr, :w] += dk
                 g_t[vr, :w] += dv
             outs += [(dq * sc).astype(bf), (g_t[kr, rows] * sc).astype(bf), g_t[vr, rows].astype(bf)]
-        res = jnp.concatenate(outs, 0).T
-        out_ref[loc, :] = res
-        full_ref[loc, :] = res
+        full_ref[loc, :] = jnp.concatenate(outs, 0).T
+    half = (r1 - r0) // 2
+    own_ref[...] = full_ref[pl.ds(pl.multiple_of(ids[0] * half, half), half), :]
+    other_ref[...] = full_ref[pl.ds(pl.multiple_of((1 - ids[0]) * half, half), half), :]
     if has_out:
         acc_out[0] = g_t[:, :r0]
 
 
-def _attn_bwd(qkv, tr, o, do, lse, acc, full, chunk, b, hd):
+def _attn_bwd(ids, qkv, tr, o, do, lse, acc, full, chunk, b, hd):
     t, w = qkv.shape
     npair = w // (6 * hd)
     r0, r1 = chunk * b, (chunk + 1) * b
     has_in, has_out = acc is not None, r0 > 0
     in_specs = [
-        pl.BlockSpec((b, 6 * hd), lambda p: (chunk, p)),
-        pl.BlockSpec((1, 6 * hd, r1), lambda p: (p, 0, 0)),
-        pl.BlockSpec((b, 2 * hd), lambda p: (chunk, p)),
-        pl.BlockSpec((b, 2 * hd), lambda p: (0, p)),
-        pl.BlockSpec((1, 2, t), lambda p: (p, 0, 0)),
+        pl.BlockSpec((b, 6 * hd), lambda p, s: (chunk, p)),
+        pl.BlockSpec((1, 6 * hd, r1), lambda p, s: (p, 0, 0)),
+        pl.BlockSpec((b, 2 * hd), lambda p, s: (chunk, p)),
+        pl.BlockSpec((b, 2 * hd), lambda p, s: (0, p)),
+        pl.BlockSpec((1, 2, t), lambda p, s: (p, 0, 0)),
     ]
     args = [qkv, tr, o, do, lse]
     alias = {}
     if has_in:
-        in_specs += [pl.BlockSpec((1, 4 * hd, r1), lambda p: (p, 0, 0)), pl.BlockSpec(memory_space=pl.ANY)]
+        in_specs += [pl.BlockSpec((1, 4 * hd, r1), lambda p, s: (p, 0, 0)), pl.BlockSpec(memory_space=pl.ANY)]
         args += [acc, full]
-        alias = {6: 1}
-    out_specs = [pl.BlockSpec((b, 6 * hd), lambda p: (0, p)), pl.BlockSpec((b, 6 * hd), lambda p: (chunk, p))]
-    out_shape = [jax.ShapeDtypeStruct((b, w), bf), jax.ShapeDtypeStruct((t, w), bf)]
+        alias = {7: 2}
+    out_specs = [pl.BlockSpec((b // 2, 6 * hd), lambda p, s: (0, p))] * 2 + [pl.BlockSpec((b, 6 * hd), lambda p, s: (chunk, p))]
+    out_shape = [jax.ShapeDtypeStruct((b // 2, w), bf)] * 2 + [jax.ShapeDtypeStruct((t, w), bf)]
     if has_out:
-        out_specs.append(pl.BlockSpec((1, 4 * hd, r0), lambda p: (p, 0, 0)))
+        out_specs.append(pl.BlockSpec((1, 4 * hd, r0), lambda p, s: (p, 0, 0)))
         out_shape.append(jax.ShapeDtypeStruct((npair, 4 * hd, r0), f32))
     work = npair * 2 * b * (r0 + r1)
     return pl.pallas_call(
         functools.partial(_bwd_kernel, hd=hd, r0=r0, r1=r1, has_in=has_in, has_out=has_out),
-        grid=(npair,),
-        in_specs=in_specs,
-        out_specs=out_specs,
+        grid_spec=pltpu.PrefetchScalarGridSpec(
+            num_scalar_prefetch=1,
+            grid=(npair,),
+            in_specs=in_specs,
+            out_specs=out_specs,
+            scratch_shapes=[pltpu.VMEM((4 * hd, r1), f32)],
+        ),
         out_shape=out_shape,
-        scratch_shapes=[pltpu.VMEM((4 * hd, r1), f32)],
         input_output_aliases=alias,
         compiler_params=_params(),
         cost_estimate=_cost(work * 1500, 3 * t * w),
-    )(*args)
+    )(ids, *args)
 
 
 def _h1_kernel(ids, x_ref, oa, ob, pa, pb, qa, qb, ra, rb, wa, wb, wc, wd, g_ref, xh_ref, rs_ref, own_ref, full_ref, acc):
     def run(first, second):
         acc[...] = sum(_dot(jnp.concatenate([u, v], 1), w[...]) for u, v, w in first + second)
 
-    near = [(oa[0, 0], ob[0, 0], wa), (pa[0], pb[0], wb)]
-    far = [(qa[0, 0], qb[0, 0], wc), (ra[0], rb[0], wd)]
+    near = [(oa[0, 0], ob[0, 0], wa), (pa[0, 0], pb[0, 0], wb)]
+    far = [(qa[0, 0], qb[0, 0], wc), (ra[0, 0], rb[0, 0], wd)]
 
     @pl.when(ids[1] == 0)
     def _():
@@ -226,7 +230,6 @@
 def _h1(ids, chunk, x4, o_own, o_same, o_cross, o_diag, ws, g2):
     _, _, r, d = x4.shape
     own = lambda k: pl.BlockSpec((1, 1, TILE, k), lambda i, s: (chunk, s[0], i, 0))
-    row = lambda k: pl.BlockSpec((1, TILE, k), lambda i, s: (chunk, i, 0))
     flat = lambda k: pl.BlockSpec((TILE, k), lambda i, s: (i, 0))
     const = lambda shape: pl.BlockSpec(shape, lambda i, s: (0, 0), pipeline_mode=pl.Buffered(1))
     k = o_own[0].shape[-1]
@@ -235,7 +238,7 @@
         grid_spec=pltpu.PrefetchScalarGridSpec(
             num_scalar_prefetch=1,
             grid=(r // TILE,),
-            in_specs=[own(d), own(k), own(k), row(k), row(k), own(k), own(k), row(k), row(k)]
+            in_specs=[own(d)] + [own(k)] * 8
             + [const((2 * k, d))] * 4
             + [const((1, d))],
             out_specs=[flat(d), flat(128), flat(d), pl.BlockSpec((1, TILE, d), lambda i, s: (s[0], i, 0))],
@@ -252,6 +255,50 @@
     )(ids, x4, *o_own, *o_same, *o_cross, *o_diag, *ws, g2)
 
 
+GC0 = 0.7978845608028654
+GC1 = 0.044715
+
+
+def _mlp_kernel(ids, n_ref, w_ref, dg_ref, *refs):
+    gl_ref, da_ref, own_ref, other_ref = refs[-4:]
+    sub = own_ref.shape[0]
+    for half in range(2):
+        rows = slice(half * sub, half * sub + sub)
+        a = _dot(n_ref[rows, :], w_ref[...])
+        a2 = a * a
+        h = 0.5 + 0.5 * jnp.tanh(a * (GC0 + GC0 * GC1 * a2))
+        gl_ref[rows, :] = (a * h).astype(bf)
+        slope = h + a * (2.0 * h * (1.0 - h)) * (GC0 + 3.0 * GC0 * GC1 * a2)
+        da_ref[rows, :] = (dg_ref[rows, :] * slope).astype(bf)
+    own_ref[...] = da_ref[pl.ds(pl.multiple_of(ids[0] * sub, sub), sub), :]
+    other_ref[...] = da_ref[pl.ds(pl.multiple_of((1 - ids[0]) * sub, sub), sub), :]
+
+
+def _mlp(ids, n2, w1, dg, chunk, prev, bn=512):
+    b, d = n2.shape
+    t, f = dg.shape
+    spec = pl.BlockSpec((b, bn), lambda j, s: (chunk, j))
+    half = pl.BlockSpec((b // 2, bn), lambda j, s: (0, j))
+    return pl.pallas_call(
+        _mlp_kernel,
+        grid_spec=pltpu.PrefetchScalarGridSpec(
+            num_scalar_prefetch=1,
+            grid=(f // bn,),
+            in_specs=[
+                pl.BlockSpec((b, d), lambda j, s: (0, 0), pipeline_mode=pl.Buffered(1)),
+                pl.BlockSpec((d, bn), lambda j, s: (0, j)),
+                spec,
+            ]
+            + [pl.BlockSpec(memory_space=pl.ANY)] * len(prev),
+            out_specs=[spec, spec, half, half],
+        ),
+        out_shape=[jax.ShapeDtypeStruct((t, f), bf)] * 2 + [jax.ShapeDtypeStruct((b // 2, f), bf)] * 2,
+        input_output_aliases={4: 0, 5: 1} if prev else {},
+        compiler_params=_params(),
+        cost_estimate=_cost(2 * b * d * f * 1.3, 2 * b * f * 8),
+    )(ids, n2, w1, dg, *prev)
+
+
 def _place_kernel(ids, v_ref, _, buf_ref):
     buf_ref[0] = v_ref[...]
 
@@ -268,7 +315,7 @@
         ),
         out_shape=jax.ShapeDtypeStruct(buf.shape, buf.dtype),
         input_output_aliases={2: 0},
-        compiler_params=_params(32),
+        compiler_params=_params(),
         cost_estimate=_cost(r * d * 1000, 2 * r * d * 2),
     )(ids, v, buf)
 
@@ -289,7 +336,7 @@
         ),
         out_shape=jax.ShapeDtypeStruct(buf.shape, buf.dtype),
         input_output_aliases={2: 0},
-        compiler_params=_params(32),
+        compiler_params=_params(),
         cost_estimate=_cost(r * d * 1000, 2 * r * d * 2),
     )(ids, v, buf)
 
@@ -335,7 +382,7 @@
         ),
         out_shape=outs,
         input_output_aliases=alias or {},
-        compiler_params=_params(32),
+        compiler_params=_params(),
         cost_estimate=_cost(r * 2048 * 6000, r * 2048 * 16),
     )(ids, *args)
 
@@ -371,7 +418,6 @@
             return lax.ppermute(v, "tp", CROSS)
 
         split = lambda v: v.reshape(NB, 2, r, v.shape[-1])
-        pick = lambda v, c: lax.dynamic_index_in_dim(v, c, v.ndim - 3, keepdims=False)
         sds = jax.ShapeDtypeStruct
         order = _Chain()
         tie, did = order.tie, order.did
@@ -395,8 +441,8 @@
             oc = cross(o)
             o_own.append(split(o))
             o_cross.append(split(oc))
-            o_same.append(same(pick(split(o), 1 - core)))
-            o_diag.append(same(pick(split(oc), 1 - core)))
+            o_same.append(split(same(o)))
+            o_diag.append(split(same(oc)))
         o_all, lse, qkv_t = prev
 
         dg = did(_dot_t(tie(dy), w2))
@@ -410,41 +456,28 @@
             did(own)
             others[k] = same(own)
 
-        gl, da, sums, n2f = [None] * NB, [None] * NB, [None] * NB, [None] * NB
-        dyc = dy.reshape(NB, b, d)
-        dgc = dg.reshape(NB, b, -1)
+        sums, n2f = [None] * NB, [None] * NB
 
         def place_n2(k):
             n2f[k] = did(_place(ids, tie(n2[k]), others[k])).reshape(b, d)
 
-        def mlp(k):
-            a = _dot(tie(n2f[k]), w1)
-            g, gelu_vjp = jax.vjp(jax.nn.gelu, a)
-            gl[k] = g.astype(bf)
-            da[k] = did(gelu_vjp(dgc[k])[0].astype(bf))
+        def mlp(k, prev):
+            res = _mlp(ids, tie(n2f[k]), w1, dg, k, prev)
+            did(res[1])
+            return res
 
         def partial_other(v, w):
-            p = did(_dot_t(pick(tie(v).reshape(2, r, -1), 1 - core), w).astype(bf))
+            p = did(_dot_t(tie(v), w).astype(bf))
             return same(p)
 
         def partial_own(v, w, recv):
-            s_own = did((_dot_t(pick(tie(v).reshape(2, r, -1), core), w) + recv.astype(f32)).astype(bf))
+            s_own = did((_dot_t(tie(v), w) + recv.astype(f32)).astype(bf))
             return s_own, cross(s_own)
 
         def grad(u, v, add=None, keep=False):
-            p = _dot(tie(u).T, v)
+            p = _dot(u.T, tie(v))
             p = p if add is None else p + add
             return did(p if keep else p.astype(bf))
-
-        place_n2(1)
-        mlp(1)
-        recv = partial_other(da[1], w1)
-        place_n2(0)
-        sums[1] = partial_own(da[1], w1, recv)
-        mlp(0)
-        recv = partial_other(da[0], w1)
-        dw2 = grad(gl[1], dyc[1], keep=True)
-        sums[0] = partial_own(da[0], w1, recv)
 
         dh, dhb = [None] * NB, [None] * NB
 
@@ -460,7 +493,7 @@
         def attention(k, other, acc, full):
             dhb[k] = did(_place(ids, tie(dhb[k]), other)).reshape(b, d)
             do = did(_dot_t(tie(dhb[k]), wo2).astype(bf))
-            res = _attn_bwd(qkv, qkv_t, o_all, do, lse, acc, full, k, b, hd)
+            res = _attn_bwd(ids, qkv, qkv_t, o_all, do, lse, acc, full, k, b, hd)
             did(res[0])
             return res
 
@@ -474,22 +507,30 @@
             did(own)
             return same(own), dx
 
+        place_n2(1)
+        *gd, da_own, da_other = mlp(1, ())
+        recv = partial_other(da_other, w1)
+        place_n2(0)
+        sums[1] = partial_own(da_own, w1, recv)
+        gl, da, da_own, da_other = mlp(0, gd)
+        recv = partial_other(da_other, w1)
+        dw2 = grad(gl, dy)
+        other = norm2(1)
+        sums[0] = partial_own(da_own, w1, recv)
+
         mu4, rs4 = mu1.reshape(NB, 2, 1, r), rs1.reshape(NB, 2, 1, r)
         o3 = o_all.reshape(NB, b, -1)
 
-        other = norm2(1)
-        dw2 = grad(gl[0], dyc[0], dw2)
-        dq1, full, acc = attention(1, other, None, None)
-        recv = partial_other(dq1, wqkv)
+        own1, oth1, full, acc = attention(1, other, None, None)
+        recv = partial_other(oth1, wqkv)
         other = norm2(0)
-        pair1 = partial_own(dq1, wqkv, recv)
-        dq0, full = attention(0, other, acc, full)
-        recv = partial_other(dq0, wqkv)
+        pair1 = partial_own(own1, wqkv, recv)
+        own0, oth0, full = attention(0, other, acc, full)
+        recv = partial_other(oth0, wqkv)
         dwo = grad(o3[1], dhb[1], keep=True)
-        pair0 = partial_own(dq0, wqkv, recv)
+        pair0 = partial_own(own0, wqkv, recv)
         dwo = grad(o3[0], dhb[0], dwo).reshape(hl, hd, d)
-        dw1 = grad(n2f[1], da[1], keep=True)
-        dw1 = grad(n2f[0], da[0], dw1)
+        dw1 = grad(jnp.concatenate(n2f, 0), da)
         other1, dx = norm1(1, pair1, None)
         dwqkv = grad(n1, full)
         other0, dx = norm1(0, pair0, dx)

time: 527 us -> 511 us (0.970)
  Pallas kernels: 154 us -> 218 us
  matrix products: 231 us -> 194 us
  local copies, waits for them, and re-layouts: 23.2 us -> 4.53 us
  waiting for transfers between devices: 87.9 us -> 71.3 us
  other arithmetic: 10.1 us -> 1.34 us
    dot_general x10 -> x6, matrix products: 139 us -> 90.8 us  [_dot(): return jnp.dot(a, b, preferred_element_type=f32)]
    pallas_call x0 -> x2, Pallas kernels: none -> 40.4 us  [_mlp(): pl.pallas_call(_mlp_kernel, grid_spec=pltpu.PrefetchScalarGridSpec(num_sc...]
    ppermute x7, waiting for transfers between devices: 85.7 us -> 69.6 us  [cross(): return lax.ppermute(v, 'tp', CROSS)]
    unnamed x86 -> x48, local copies, waits for them, and re-layouts: 16.8 us -> 3.33 us
    pallas_call x4, Pallas kernels: 23.4 us -> 35.6 us  [_lnb(): pl.pallas_call(kernel, grid_spec=pltpu.PrefetchScalarGridSpec(num_scalar_...]
    dot_general x11, matrix products: 92.6 us -> 104 us  [_dot_t(): lax.dot_general(a, b, (((1,), (1,)), ((), ())), preferred_element_type=f32)]
    pallas_call x4, Pallas kernels: 5.05 us -> 13.8 us  [_place(): pl.pallas_call(_place_kernel, grid_spec=pltpu.PrefetchScalarGridSpec(num_...]
    convert_element_type x2 -> x1, other arithmetic: 9.39 us -> 0.69 us  [body(): n1 = ((xf - mu1[:, None]) * rs1[:, None] * g1.astype(f32)).astype(bf)]
  transfers between devices with their start and end apart: 23 -> 23, of which waited for: 6 -> 6; matrix products, arithmetic and copies ran while one was open for 39% -> 35% of each run, Pallas kernels for 23% -> 36%
where the time goes in v1:
time: 511 us; the launch traced here: 503 us
  Pallas kernels  218 us (43%)
  matrix products  194 us (38%)
  waiting for transfers between devices  71.3 us (14%)
  starting transfers between devices  11.4 us (2%)
    dot_general x11, matrix products, _dot_t(): lax.dot_general(a, b, (((1,), (1,)), ((), ())), preferred_element_type=f32)  104 us
    dot_general x6, matrix products, _dot(): return jnp.dot(a, b, preferred_element_type=f32)  90.8 us
    ppermute x7, waiting for transfers between devices, cross(): return lax.ppermute(v, 'tp', CROSS)  69.6 us
    pallas_call x2, Pallas kernels, _attn_bwd(): pl.pallas_call(functools.partial(_bwd_kernel, hd=hd, r0=r0, r1=r1, has_in...  57.7 us
    pallas_call x2, Pallas kernels, _mlp(): pl.pallas_call(_mlp_kernel, grid_spec=pltpu.PrefetchScalarGridSpec(num_sc...  40.4 us
    pallas_call x2, Pallas kernels, _attn_fwd(): pl.pallas_call(functools.partial(_fwd_kernel, t=t, hd=hd, first=prev is N...  36.9 us
    pallas_call x4, Pallas kernels, _lnb(): pl.pallas_call(kernel, grid_spec=pltpu.PrefetchScalarGridSpec(num_scalar_...  35.6 us
    pallas_call x2, Pallas kernels, _h1(): pl.pallas_call(_h1_kernel, grid_spec=pltpu.PrefetchScalarGridSpec(num_sca...  27.1 us
  transfers between devices with their start and end apart: 23, of which 6 were waited for; matrix products, arithmetic and copies ran while one was open for 35% of the time, Pallas kernels for 36%

profile of v1, /device:TPU:0, one launch (start us, length us, event | category | flops | bytes accessed | tf_op | source)
XLA Modules:
  0.0 502.6 jit_solution(12772350363061557190)
XLA Ops:
  0.6 3.3 collective-permute-start.7
  4.0 0.7 convert_element_type.67
  5.2 19.0 %convolution_convert_fusion.1.refs_0_.refs_1_ = bf16[2048,1536]{1,0:T(8,128)(2,1)} fusion(bf16[2048,1536]{1,0:T(8,128)(2,1)} %param.16, bf16[2048,2048]{1,0:T(8,128)(2,1)} %param.10, f32[2048]{0:T(1024)S(1)} %convert_element_type.67, f32[2048]{0:T(1024)} %param.12, f32[2048]{0:T(1024)} %param.11), kind=kOutput, calls=%fused_computation.7 | convolution fusion | flops 12909019136 | bytes 20996096 | tf_op jit(solution)/shard_map/dot_general | solution.py:24
  24.3 18.2 %attn_fwd.2 = (bf16[2048,256]{1,0:T(8,128)(2,1)}, bf16[2048,512]{1,0:T(8,128)(2,1)}, f32[4,2,2048]{2,1,0:T(2,128)}, bf16[4,384,2048]{2,1,0:T(8,128)(2,1)}) custom-call(bf16[2048,1536]{1,0:T(8,128)(2,1)} %convolution_convert_fusion.1.refs_0_.refs_1_), custom_call_target="tpu_custom_call" | custom-call | flops 19000000512 | bytes 8388608 | tf_op jit(solution)/shard_map/attn_fwd/pallas_call | solution.py:81
  42.5 18.7 %attn_fwd.3 = (bf16[2048,256]{1,0:T(8,128)(2,1)}, bf16[2048,512]{1,0:T(8,128)(2,1)}, f32[4,2,2048]{2,1,0:T(2,128)}, bf16[4,384,2048]{2,1,0:T(8,128)(2,1)}) custom-call(bf16[2048,1536]{1,0:T(8,128)(2,1)} %convolution_convert_fusion.1.refs_0_.refs_1_, ...), custom_call_target="tpu_custom_call", output_to_operand_aliasing={{1}: (1, {}), {2}: (2, {}), {3}: (3, {})} | custom-call | flops 19000000512 | bytes 8388608 | tf_op jit(solution)/shard_map/attn_fwd/pallas_call | solution.py:81
  61.3 2.0 collective-permute-start.2
  63.5 24.1 %collective-permute-done.3 = bf16[2048,256]{1,0:T(8,128)(2,1)} collective-permute-done((bf16[2048,256]{1,0:T(8,128)(2,1)}, bf16[2048,256]{1,0:T(8,128)(2,1)}, u32[]{:S(2)}, u32[]{:S(2)}) %collective-permute-start.3) | collective-permute-done | bytes 1048608 | tf_op jit(solution)/shard_map/ppermute | solution.py:418
  88.1 20.6 %collective-permute-done.2 = bf16[2048,256]{1,0:T(8,128)(2,1)} collective-permute-done((bf16[2048,256]{1,0:T(8,128)(2,1)S(1)}, bf16[2048,256]{1,0:T(8,128)(2,1)}, u32[]{:S(2)}, u32[]{:S(2)}) %collective-permute-start.2) | collective-permute-done | bytes 1048608 | tf_op jit(solution)/shard_map/ppermute | solution.py:418
  109.2 24.8 %fusion.11.dg_ref = f32[2048,2048]{1,0:T(8,128)} fusion(bf16[2048,2048]{1,0:T(8,128)(2,1)} %param.15, bf16[2048,2048]{1,0:T(8,128)(2,1)} %param.19), kind=kOutput, calls=%fused_computation.25 | convolution fusion | flops 17179869184 | bytes 33554432 | tf_op jit(solution)/shard_map/dot_general | solution.py:28
  135.2 13.5 %shard_map.137 = (f32[512,2048]{1,0:T(8,128)}, f32[512,128]{1,0:T(8,128)}, bf16[512,2048]{1,0:T(8,128)(2,1)}, bf16[2,512,2048]{2,1,0:T(8,128)(2,1)}) custom-call(s32[2]{0:T(128)} %pad_add_fusion.ids.refs_0_, bf16[2,2,512,2048]{3,2,1,0:T(8,128)(2,1)} %bitcast.50, bf16[2,2,512,256]{3,2,1,0:T(8,128)(2,1)} %bitcast.69, bf16[2,2,512,256]{3,2,1,0:T(8,128)(2,1)} %bitcast.71, ...), custom_call_target="tpu_custom_call" | custom-call | flops 4294967296 | bytes 20971520 | tf_op jit(solution)/shard_map/pallas_call | solution.py:236
  148.8 13.6 %shard_map.138 = (f32[512,2048]{1,0:T(8,128)}, f32[512,128]{1,0:T(8,128)}, bf16[512,2048]{1,0:T(8,128)(2,1)}, bf16[2,512,2048]{2,1,0:T(8,128)(2,1)}) custom-call(s32[2]{0:T(128)} %pad_add_fusion.ids.refs_0_, bf16[2,2,512,2048]{3,2,1,0:T(8,128)(2,1)} %bitcast.51, bf16[2,2,512,256]{3,2,1,0:T(8,128)(2,1)} %bitcast.70, bf16[2,2,512,256]{3,2,1,0:T(8,128)(2,1)} %bitcast.72, ...), custom_call_target="tpu_custom_call" | custom-call | flops 4294967296 | bytes 20971520 | tf_op jit(solution)/shard_map/pallas_call | solution.py:236
  162.9 1.3 copy-done.10
  164.2 3.3 shard_map.139
  167.5 20.2 %shard_map.140 = (bf16[2048,2048]{1,0:T(8,128)(2,1)}, bf16[2048,2048]{1,0:T(8,128)(2,1)}, bf16[512,2048]{1,0:T(8,128)(2,1)}, bf16[512,2048]{1,0:T(8,128)(2,1)}) custom-call(s32[2]{0:T(128)} %pad_add_fusion.ids.refs_0_, bf16[1024,2048]{1,0:T(8,128)(2,1)} %bitcast.75, bf16[2048,2048]{1,0:T(8,128)(2,1)} %w_ref.3, f32[2048,2048]{1,0:T(8,128)} %fusion.11.dg_ref), custom_call_target="tpu_custom_call" | custom-call | flops 11166914560 | bytes 33554432 | tf_op jit(solution)/shard_map/pallas_call | solution.py:282
  187.7 8.5 %convolution_convert_fusion.6 = bf16[512,2048]{1,0:T(8,128)(2,1)S(1)} fusion(bf16[512,2048]{1,0:T(8,128)(2,1)} %get-tuple-element.96, bf16[2048,2048]{1,0:T(8,128)(2,1)} %w_ref.3), kind=kOutput, calls=%fused_computation.17 | convolution fusion | flops 4296015872 | bytes 12582912 | tf_op jit(solution)/shard_map/dot_general | solution.py:28
  196.3 3.4 shard_map.141
  199.7 0.8 collective-permute-done.11
  200.5 9.1 %add_convert_fusion.4.sa = bf16[512,2048]{1,0:T(8,128)(2,1)S(1)} fusion(bf16[512,2048]{1,0:T(8,128)(2,1)} %collective-permute-done.11, bf16[512,2048]{1,0:T(8,128)(2,1)} %get-tuple-element.99, bf16[2048,2048]{1,0:T(8,128)(2,1)} %w_ref.3), kind=kOutput, calls=%fused_computation.13 | convolution fusion | flops 4298113024 | bytes 14680064 | tf_op jit(solution)/shard_map/dot_general | solution.py:28
  210.0 20.2 %shard_map.142 = (bf16[2048,2048]{1,0:T(8,128)(2,1)}, bf16[2048,2048]{1,0:T(8,128)(2,1)}, bf16[512,2048]{1,0:T(8,128)(2,1)}, bf16[512,2048]{1,0:T(8,128)(2,1)}) custom-call(s32[2]{0:T(128)} %pad_add_fusion.ids.refs_0_, bf16[1024,2048]{1,0:T(8,128)(2,1)} %bitcast.57, bf16[2048,2048]{1,0:T(8,128)(2,1)} %w_ref.3, ...), custom_call_target="tpu_custom_call", output_to_operand_aliasing={{0}: (4, {}), {1}: (5, {})} | custom-call | flops 11166914560 | bytes 33554432 | tf_op jit(solution)/shard_map/pallas_call | solution.py:282
  230.2 10.0 %convolution_convert_fusion.5 = bf16[512,2048]{1,0:T(8,128)(2,1)} fusion(bf16[512,2048]{1,0:T(8,128)(2,1)} %get-tuple-element.106, bf16[2048,2048]{1,0:T(8,128)(2,1)} %w_ref.3), kind=kOutput, calls=%fused_computation.16 | convolution fusion | flops 4296015872 | bytes 12582912 | tf_op jit(solution)/shard_map/dot_general | solution.py:28
  240.2 22.2 %convolution_convert_fusion = bf16[2048,2048]{1,0:T(8,128)(2,1)} fusion(bf16[2048,2048]{1,0:T(8,128)(2,1)S(1)} %copy-done.5, bf16[2048,2048]{1,0:T(8,128)(2,1)} %param.15), kind=kOutput, calls=%fused_computation.6 | convolution fusion | flops 17184063488 | bytes 25165824 | tf_op jit(solution)/shard_map/dot_general | solution.py:24
  262.4 9.2 %shard_map.143 = (f32[512,2048]{1,0:T(8,128)}, bf16[512,2048]{1,0:T(8,128)(2,1)}, bf16[2,512,2048]{2,1,0:T(8,128)(2,1)}) custom-call(s32[2]{0:T(128)} %pad_add_fusion.ids.refs_0_, bf16[512,2048]{1,0:T(8,128)(2,1)} %copy-done.19, bf16[512,2048]{1,0:T(8,128)(2,1)} %collective-permute-done.12.sb, f32[512,2048]{1,0:T(8,128)} %get-tuple-element.109.xh_ref, ...), custom_call_target="tpu_custom_call" | custom-call | flops 6291456000 | bytes 16777216 | tf_op jit(solution)/shard_map/pallas_call | solution.py:375
  272.1 9.4 %add_convert_fusion.3.sa = bf16[512,2048]{1,0:T(8,128)(2,1)} fusion(bf16[512,2048]{1,0:T(8,128)(2,1)} %collective-permute-done.13, bf16[512,2048]{1,0:T(8,128)(2,1)S(1)} %copy-done.18, bf16[2048,2048]{1,0:T(8,128)(2,1)} %w_ref.3), kind=kOutput, calls=%fused_computation.12 | convolution fusion | flops 4298113024 | bytes 14680064 | tf_op jit(solution)/shard_map/dot_general | solution.py:28
  281.5 1.7 collective-permute-start.15
  283.3 3.8 shard_map.144
  287.1 5.6 %convolution_convert_fusion.8.refs_4_ = bf16[1024,512]{1,0:T(8,128)(2,1)} fusion(bf16[1024,2048]{1,0:T(8,128)(2,1)} %bitcast.55, bf16[512,2048]{1,0:T(8,128)(2,1)S(1)} %bitcast.65), kind=kOutput, calls=%fused_computation.19 | convolution fusion | flops 2148007936 | bytes 7340032 | tf_op jit(solution)/shard_map/dot_general | solution.py:28
  292.7 38.7 %shard_map.145 = (bf16[512,1536]{1,0:T(8,128)(2,1)}, bf16[512,1536]{1,0:T(8,128)(2,1)}, bf16[2048,1536]{1,0:T(8,128)(2,1)}, f32[4,256,1024]{2,1,0:T(8,128)}) custom-call(s32[2]{0:T(128)} %pad_add_fusion.ids.refs_0_, bf16[2048,1536]{1,0:T(8,128)(2,1)} %convolution_convert_fusion.1.refs_0_.refs_1_, bf16[4,384,2048]{2,1,0:T(8,128)(2,1)} %get-tuple-element.82.refs_2_, ...), custom_call_target="tpu_custom_call" | custom-call | flops 37748736000 | bytes 9437184 | tf_op jit(solution)/shard_map/pallas_call | solution.py:188
  331.4 8.0 %convolution_convert_fusion.4 = bf16[512,2048]{1,0:T(8,128)(2,1)} fusion(bf16[512,1536]{1,0:T(8,128)(2,1)} %get-tuple-element.119, bf16[2048,1536]{1,0:T(8,128)(2,1)} %param.16), kind=kOutput, calls=%fused_computation.15 | convolution fusion | flops 3222274048 | bytes 9961472 | tf_op jit(solution)/shard_map/dot_general | solution.py:28
  339.5 9.4 %shard_map.146 = (f32[512,2048]{1,0:T(8,128)}, bf16[512,2048]{1,0:T(8,128)(2,1)}, bf16[2,512,2048]{2,1,0:T(8,128)(2,1)}) custom-call(s32[2]{0:T(128)} %pad_add_fusion.ids.refs_0_, bf16[512,2048]{1,0:T(8,128)(2,1)} %add_convert_fusion.3.sa, bf16[512,2048]{1,0:T(8,128)(2,1)} %collective-permute-done.15.sb, f32[512,2048]{1,0:T(8,128)} %get-tuple-element.121.xh_ref, ...), custom_call_target="tpu_custom_call" | custom-call | flops 6291456000 | bytes 16777216 | tf_op jit(solution)/shard_map/pallas_call | solution.py:375
  349.3 7.8 %add_convert_fusion.2.sa = bf16[512,2048]{1,0:T(8,128)(2,1)} fusion(bf16[512,2048]{1,0:T(8,128)(2,1)} %collective-permute-done.17, bf16[512,1536]{1,0:T(8,128)(2,1)S(1)} %copy-done.20, bf16[2048,1536]{1,0:T(8,128)(2,1)} %param.16), kind=kOutput, calls=%fused_computation.11 | convolution fusion | flops 3224371200 | bytes 12058624 | tf_op jit(solution)/shard_map/dot_general | solution.py:28
  357.1 3.3 shard_map.147
  360.4 5.5 %convolution_convert_fusion.7.refs_4_ = bf16[1024,512]{1,0:T(8,128)(2,1)} fusion(bf16[1024,2048]{1,0:T(8,128)(2,1)} %bitcast.59, bf16[512,2048]{1,0:T(8,128)(2,1)S(1)} %bitcast.66), kind=kOutput, calls=%fused_computation.18 | convolution fusion | flops 2148007936 | bytes 7340032 | tf_op jit(solution)/shard_map/dot_general | solution.py:28
  366.0 19.0 %shard_map.148 = (bf16[512,1536]{1,0:T(8,128)(2,1)}, bf16[512,1536]{1,0:T(8,128)(2,1)}, bf16[2048,1536]{1,0:T(8,128)(2,1)}) custom-call(s32[2]{0:T(128)} %pad_add_fusion.ids.refs_0_, bf16[2048,1536]{1,0:T(8,128)(2,1)} %convolution_convert_fusion.1.refs_0_.refs_1_, bf16[4,384,2048]{2,1,0:T(8,128)(2,1)} %get-tuple-element.82.refs_2_, ...), custom_call_target="tpu_custom_call", output_to_operand_aliasing={{2}: (7, {})} | custom-call | flops 12582912000 | bytes 9437184 | tf_op jit(solution)/shard_map/pallas_call | solution.py:188
  385.0 6.8 %convolution_convert_fusion.3 = bf16[512,2048]{1,0:T(8,128)(2,1)S(1)} fusion(bf16[512,1536]{1,0:T(8,128)(2,1)} %get-tuple-element.132, bf16[2048,1536]{1,0:T(8,128)(2,1)} %param.16), kind=kOutput, calls=%fused_computation.14 | convolution fusion | flops 3222274048 | bytes 9961472 | tf_op jit(solution)/shard_map/dot_general | solution.py:28
  392.8 2.4 fusion.8
  395.2 0.8 collective-permute-done.18
  396.1 8.0 %add_convert_fusion.1.sa = bf16[512,2048]{1,0:T(8,128)(2,1)} fusion(bf16[512,2048]{1,0:T(8,128)(2,1)S(1)} %collective-permute-done.18, bf16[512,1536]{1,0:T(8,128)(2,1)S(1)} %copy-done.21, bf16[2048,1536]{1,0:T(8,128)(2,1)} %param.16), kind=kOutput, calls=%fused_computation.10 | convolution fusion | flops 3224371200 | bytes 12058624 | tf_op jit(solution)/shard_map/dot_general | solution.py:28
  404.1 0.9 collective-permute-start.20
  405.0 3.9 add_convert_fusion
  408.9 20.8 %fusion.4 = bf16[2048,2048]{1,0:T(8,128)(2,1)} fusion(bf16[2048,2048]{1,0:T(8,128)(2,1)S(1)} %bitcast.68, bf16[1024,2048]{1,0:T(8,128)(2,1)S(1)} %bitcast.76, bf16[1024,2048]{1,0:T(8,128)(2,1)S(1)} %bitcast.58), kind=kOutput, calls=%fused_computation.5 | convolution fusion | flops 17200840704 | bytes 25165824 | tf_op jit(solution)/shard_map/dot_general | solution.py:24
  429.7 11.7 %collective-permute-done.19.sb = bf16[512,2048]{1,0:T(8,128)(2,1)} collective-permute-done((bf16[512,2048]{1,0:T(8,128)(2,1)}, bf16[512,2048]{1,0:T(8,128)(2,1)}, u32[]{:S(2)}, u32[]{:S(2)}) %collective-permute-start.19) | collective-permute-done | bytes 2097184 | tf_op jit(solution)/shard_map/ppermute | solution.py:418
  441.3 8.5 %shard_map.149 = (bf16[512,2048]{1,0:T(8,128)(2,1)}, bf16[2,2,512,2048]{3,2,1,0:T(8,128)(2,1)}) custom-call(s32[2]{0:T(128)} %pad_add_fusion.ids.refs_0_, bf16[512,2048]{1,0:T(8,128)(2,1)} %add_convert_fusion.2.sa, bf16[512,2048]{1,0:T(8,128)(2,1)} %collective-permute-done.19.sb, bf16[2,2,512,2048]{3,2,1,0:T(8,128)(2,1)} %bitcast.52, ...), custom_call_target="tpu_custom_call" | custom-call | flops 6291456000 | bytes 16777216 | tf_op jit(solution)/shard_map/pallas_call | solution.py:375
  449.9 22.6 %convolution_convert_fusion.2 = bf16[2048,1536]{1,0:T(8,128)(2,1)} fusion(bf16[2048,1536]{1,0:T(8,128)(2,1)} %get-tuple-element.141, bf16[2048,2048]{1,0:T(8,128)(2,1)} %param.10, f32[2048]{0:T(1024)S(1)} %copy-done.16, f32[2048]{0:T(1024)S(1)} %copy-done.13, f32[2048]{0:T(1024)S(1)} %copy-done.14), kind=kOutput, calls=%fused_computation.8 | convolution fusion | flops 12909019136 | bytes 20996096 | tf_op jit(solution)/shard_map/dot_general | solution.py:24
  472.5 13.3 %collective-permute-done.20.sb = bf16[512,2048]{1,0:T(8,128)(2,1)} collective-permute-done((bf16[512,2048]{1,0:T(8,128)(2,1)}, bf16[512,2048]{1,0:T(8,128)(2,1)}, u32[]{:S(2)}, u32[]{:S(2)}) %collective-permute-start.20) | collective-permute-done | bytes 2097184 | tf_op jit(solution)/shard_map/ppermute | solution.py:418
  485.8 8.4 %shard_map.150 = (bf16[512,2048]{1,0:T(8,128)(2,1)}, bf16[2,2,512,2048]{3,2,1,0:T(8,128)(2,1)}) custom-call(s32[2]{0:T(128)} %pad_add_fusion.ids.refs_0_, bf16[512,2048]{1,0:T(8,128)(2,1)} %add_convert_fusion.1.sa, bf16[512,2048]{1,0:T(8,128)(2,1)} %collective-permute-done.20.sb, ...), custom_call_target="tpu_custom_call", output_to_operand_aliasing={{1}: (8, {})} | custom-call | flops 6291456000 | bytes 16777216 | tf_op jit(solution)/shard_map/pallas_call | solution.py:375
  494.3 1.3 copy-done.11
  495.6 3.3 shard_map.151._
  498.9 3.3 shard_map.152
  (86 shorter events, 6.1 us)
Async XLA Ops:
  0.6 108.0 %collective-permute-start.7 = (bf16[512,2048]{1,0:T(8,128)(2,1)}, bf16[512,2048]{1,0:T(8,128)(2,1)}, u32[]{:S(2)}, u32[]{:S(2)}) collective-permute-start(bf16[512,2048]{1,0:T(8,128)(2,1)} %bitcast.61), channel_id=1, source_target_pairs={{0,2},{2,0},{1,3},{3,1},{4,6},{6,4},{5,7},{7,5}} | collective-permute-start | bytes 6291464 | tf_op jit(solution)/shard_map/ppermute | solution.py:418
  4.6 0.6 copy-start.15
  42.5 18.8 %copy-start.6 = (bf16[2048,256]{1,0:T(8,128)(2,1)S(1)}, bf16[2048,256]{1,0:T(8,128)(2,1)}, u32[]{:S(2)}) copy-start(bf16[2048,256]{1,0:T(8,128)(2,1)} %get-tuple-element.77) | copy-start | bytes 3145732
  42.5 45.1 %copy-start.3 = (bf16[8,64,2048]{2,1,0:T(8,128)(2,1)S(1)}, bf16[8,64,2048]{2,1,0:T(8,128)(2,1)}, u32[]{:S(2)}) copy-start(bf16[8,64,2048]{2,1,0:T(8,128)(2,1)} %param.17) | copy-start | bytes 6291460
  61.2 72.8 %copy-start.17 = (bf16[2048]{0:T(1024)(128)(2,1)S(1)}, bf16[2048]{0:T(1024)(128)(2,1)}, u32[]{:S(2)}) copy-start(bf16[2048]{0:T(1024)(128)(2,1)} %param.14) | copy-start | bytes 12292
  61.2 26.4 %collective-permute-start.3 = (bf16[2048,256]{1,0:T(8,128)(2,1)}, bf16[2048,256]{1,0:T(8,128)(2,1)}, u32[]{:S(2)}, u32[]{:S(2)}) collective-permute-start(bf16[2048,256]{1,0:T(8,128)(2,1)} %get-tuple-element.84), channel_id=1, source_target_pairs={{0,2},{2,0},{1,3},{3,1},{4,6},{6,4},{5,7},{7,5}} | collective-permute-start | bytes 3145736 | tf_op jit(solution)/shard_map/ppermute | solution.py:418
  61.2 26.3 %collective-permute-start.1 = (bf16[2048,256]{1,0:T(8,128)(2,1)}, bf16[2048,256]{1,0:T(8,128)(2,1)S(1)}, u32[]{:S(2)}, u32[]{:S(2)}) collective-permute-start(bf16[2048,256]{1,0:T(8,128)(2,1)} %get-tuple-element.84), channel_id=1, source_target_pairs={{0,1},{1,0},{2,3},{3,2},{4,5},{5,4},{6,7},{7,6}} | collective-permute-start | bytes 3145736 | tf_op jit(solution)/shard_map/ppermute | solution.py:415
  61.3 47.4 %collective-permute-start.2 = (bf16[2048,256]{1,0:T(8,128)(2,1)S(1)}, bf16[2048,256]{1,0:T(8,128)(2,1)}, u32[]{:S(2)}, u32[]{:S(2)}) collective-permute-start(bf16[2048,256]{1,0:T(8,128)(2,1)S(1)} %copy-done.6), channel_id=1, source_target_pairs={{0,2},{2,0},{1,3},{3,1},{4,6},{6,4},{5,7},{7,5}} | collective-permute-start | bytes 3145736 | tf_op jit(solution)/shard_map/ppermute | solution.py:418
  63.2 72.0 %collective-permute-start = (bf16[2048,256]{1,0:T(8,128)(2,1)S(1)}, bf16[2048,256]{1,0:T(8,128)(2,1)}, u32[]{:S(2)}, u32[]{:S(2)}) collective-permute-start(bf16[2048,256]{1,0:T(8,128)(2,1)S(1)} %copy-done.6), channel_id=1, source_target_pairs={{0,1},{1,0},{2,3},{3,2},{4,5},{5,4},{6,7},{7,6}} | collective-permute-start | bytes 3145736 | tf_op jit(solution)/shard_map/ppermute | solution.py:415
  87.6 47.7 %collective-permute-start.6 = (bf16[512,2048]{1,0:T(8,128)(2,1)S(1)}, bf16[512,2048]{1,0:T(8,128)(2,1)}, u32[]{:S(2)}, u32[]{:S(2)}) collective-permute-start(bf16[512,2048]{1,0:T(8,128)(2,1)S(1)} %bitcast.64), channel_id=1, source_target_pairs={{0,1},{1,0},{2,3},{3,2},{4,5},{5,4},{6,7},{7,6}} | collective-permute-start | bytes 6291464 | tf_op jit(solution)/shard_map/ppermute | solution.py:415
  87.6 21.1 %copy-start.7 = (bf16[2048,256]{1,0:T(8,128)(2,1)}, bf16[2048,256]{1,0:T(8,128)(2,1)S(1)}, u32[]{:S(2)}) copy-start(bf16[2048,256]{1,0:T(8,128)(2,1)S(1)} %collective-permute-done.1) | copy-start | bytes 3145732
  87.6 47.6 %collective-permute-start.5 = (bf16[2048,256]{1,0:T(8,128)(2,1)}, bf16[2048,256]{1,0:T(8,128)(2,1)}, u32[]{:S(2)}, u32[]{:S(2)}) collective-permute-start(bf16[2048,256]{1,0:T(8,128)(2,1)} %collective-permute-done.3), channel_id=1, source_target_pairs={{0,1},{1,0},{2,3},{3,2},{4,5},{5,4},{6,7},{7,6}} | collective-permute-start | bytes 3145736 | tf_op jit(solution)/shard_map/ppermute | solution.py:415
  108.6 26.6 %collective-permute-start.4 = (bf16[2048,256]{1,0:T(8,128)(2,1)}, bf16[2048,256]{1,0:T(8,128)(2,1)}, u32[]{:S(2)}, u32[]{:S(2)}) collective-permute-start(bf16[2048,256]{1,0:T(8,128)(2,1)} %collective-permute-done.2), channel_id=1, source_target_pairs={{0,1},{1,0},{2,3},{3,2},{4,5},{5,4},{6,7},{7,6}} | collective-permute-start | bytes 3145736 | tf_op jit(solution)/shard_map/ppermute | solution.py:415
  108.6 26.6 %collective-permute-start.8 = (bf16[512,2048]{1,0:T(8,128)(2,1)}, bf16[512,2048]{1,0:T(8,128)(2,1)}, u32[]{:S(2)}, u32[]{:S(2)}) collective-permute-start(bf16[512,2048]{1,0:T(8,128)(2,1)} %collective-permute-done.7.wc), channel_id=1, source_target_pairs={{0,1},{1,0},{2,3},{3,2},{4,5},{5,4},{6,7},{7,6}} | collective-permute-start | bytes 6291464 | tf_op jit(solution)/shard_map/ppermute | solution.py:415
  148.7 14.1 %collective-permute-start.10 = (bf16[512,2048]{1,0:T(8,128)(2,1)}, bf16[512,2048]{1,0:T(8,128)(2,1)S(1)}, u32[]{:S(2)}, u32[]{:S(2)}) collective-permute-start(bf16[512,2048]{1,0:T(8,128)(2,1)} %get-tuple-element.87), channel_id=1, source_target_pairs={{0,1},{1,0},{2,3},{3,2},{4,5},{5,4},{6,7},{7,6}} | collective-permute-start | bytes 6291464 | tf_op jit(solution)/shard_map/ppermute | solution.py:415
  162.4 33.9 %collective-permute-start.9 = (bf16[512,2048]{1,0:T(8,128)(2,1)}, bf16[512,2048]{1,0:T(8,128)(2,1)}, u32[]{:S(2)}, u32[]{:S(2)}) collective-permute-start(bf16[512,2048]{1,0:T(8,128)(2,1)} %get-tuple-element.89), channel_id=1, source_target_pairs={{0,1},{1,0},{2,3},{3,2},{4,5},{5,4},{6,7},{7,6}} | collective-permute-start | bytes 6291464 | tf_op jit(solution)/shard_map/ppermute | solution.py:415
  162.9 1.3 copy-start.10
  196.2 4.3 collective-permute-start.11
  209.6 20.6 %copy-start.19 = (bf16[512,2048]{1,0:T(8,128)(2,1)}, bf16[512,2048]{1,0:T(8,128)(2,1)S(1)}, u32[]{:S(2)}) copy-start(bf16[512,2048]{1,0:T(8,128)(2,1)S(1)} %add_convert_fusion.4.sa) | copy-start | bytes 6291460
  209.6 52.7 %collective-permute-start.12 = (bf16[512,2048]{1,0:T(8,128)(2,1)S(1)}, bf16[512,2048]{1,0:T(8,128)(2,1)}, u32[]{:S(2)}, u32[]{:S(2)}) collective-permute-start(bf16[512,2048]{1,0:T(8,128)(2,1)S(1)} %add_convert_fusion.4.sa), channel_id=1, source_target_pairs={{0,2},{2,0},{1,3},{3,1},{4,6},{6,4},{5,7},{7,5}} | collective-permute-start | bytes 6291464 | tf_op jit(solution)/shard_map/ppermute | solution.py:418
  230.2 10.0 %copy-start.5 = (bf16[2048,2048]{1,0:T(8,128)(2,1)S(1)}, bf16[2048,2048]{1,0:T(8,128)(2,1)}, u32[]{:S(2)}) copy-start(bf16[2048,2048]{1,0:T(8,128)(2,1)} %get-tuple-element.103) | copy-start | bytes 25165828
  240.2 31.9 %collective-permute-start.13 = (bf16[512,2048]{1,0:T(8,128)(2,1)}, bf16[512,2048]{1,0:T(8,128)(2,1)}, u32[]{:S(2)}, u32[]{:S(2)}) collective-permute-start(bf16[512,2048]{1,0:T(8,128)(2,1)} %convolution_convert_fusion.5), channel_id=1, source_target_pairs={{0,1},{1,0},{2,3},{3,2},{4,5},{5,4},{6,7},{7,6}} | collective-permute-start | bytes 6291464 | tf_op jit(solution)/shard_map/ppermute | solution.py:415
  262.4 9.7 %copy-start.18 = (bf16[512,2048]{1,0:T(8,128)(2,1)S(1)}, bf16[512,2048]{1,0:T(8,128)(2,1)}, u32[]{:S(2)}) copy-start(bf16[512,2048]{1,0:T(8,128)(2,1)} %get-tuple-element.112) | copy-start | bytes 6291460
  271.6 11.7 %collective-permute-start.14 = (bf16[512,2048]{1,0:T(8,128)(2,1)}, bf16[512,2048]{1,0:T(8,128)(2,1)}, u32[]{:S(2)}, u32[]{:S(2)}) collective-permute-start(bf16[512,2048]{1,0:T(8,128)(2,1)} %get-tuple-element.111), channel_id=1, source_target_pairs={{0,1},{1,0},{2,3},{3,2},{4,5},{5,4},{6,7},{7,6}} | collective-permute-start | bytes 6291464 | tf_op jit(solution)/shard_map/ppermute | solution.py:415
  281.5 57.9 %collective-permute-start.15 = (bf16[512,2048]{1,0:T(8,128)(2,1)}, bf16[512,2048]{1,0:T(8,128)(2,1)}, u32[]{:S(2)}, u32[]{:S(2)}) collective-permute-start(bf16[512,2048]{1,0:T(8,128)(2,1)} %add_convert_fusion.3.sa), channel_id=1, source_target_pairs={{0,2},{2,0},{1,3},{3,1},{4,6},{6,4},{5,7},{7,5}} | collective-permute-start | bytes 6291464 | tf_op jit(solution)/shard_map/ppermute | solution.py:418
  283.3 3.8 copy-start.4
  339.4 9.9 %collective-permute-start.17 = (bf16[512,2048]{1,0:T(8,128)(2,1)}, bf16[512,2048]{1,0:T(8,128)(2,1)}, u32[]{:S(2)}, u32[]{:S(2)}) collective-permute-start(bf16[512,2048]{1,0:T(8,128)(2,1)} %convolution_convert_fusion.4), channel_id=1, source_target_pairs={{0,1},{1,0},{2,3},{3,2},{4,5},{5,4},{6,7},{7,6}} | collective-permute-start | bytes 6291464 | tf_op jit(solution)/shard_map/ppermute | solution.py:415
  339.5 9.9 %copy-start.20 = (bf16[512,1536]{1,0:T(8,128)(2,1)S(1)}, bf16[512,1536]{1,0:T(8,128)(2,1)}, u32[]{:S(2)}) copy-start(bf16[512,1536]{1,0:T(8,128)(2,1)} %get-tuple-element.125) | copy-start | bytes 4718596
  348.8 8.3 %collective-permute-start.16 = (bf16[512,2048]{1,0:T(8,128)(2,1)}, bf16[512,2048]{1,0:T(8,128)(2,1)}, u32[]{:S(2)}, u32[]{:S(2)}) collective-permute-start(bf16[512,2048]{1,0:T(8,128)(2,1)} %get-tuple-element.123), channel_id=1, source_target_pairs={{0,1},{1,0},{2,3},{3,2},{4,5},{5,4},{6,7},{7,6}} | collective-permute-start | bytes 6291464 | tf_op jit(solution)/shard_map/ppermute | solution.py:415
  385.0 6.9 %copy-start.12 = (bf16[2048]{0:T(1024)(128)(2,1)S(1)}, bf16[2048]{0:T(1024)(128)(2,1)}, u32[]{:S(2)}) copy-start(bf16[2048]{0:T(1024)(128)(2,1)} %param.13) | copy-start | bytes 12292
  385.0 7.8 %copy-start = (bf16[2,512,2048]{2,1,0:T(8,128)(2,1)S(1)}, bf16[2,512,2048]{2,1,0:T(8,128)(2,1)}, u32[]{:S(2)}) copy-start(bf16[2,512,2048]{2,1,0:T(8,128)(2,1)} %shard_map.144) | copy-start | bytes 12582916
  385.0 7.8 %copy-start.9 = (bf16[2048,512]{1,0:T(8,128)(2,1)S(1)}, bf16[2048,512]{1,0:T(8,128)(2,1)}, u32[]{:S(2)}) copy-start(bf16[2048,512]{1,0:T(8,128)(2,1)} %get-tuple-element.83.refs_3_) | copy-start | bytes 6291460
  391.9 4.2 collective-permute-start.18
  392.5 3.5 copy-start.21
  392.5 48.8 %collective-permute-start.19 = (bf16[512,2048]{1,0:T(8,128)(2,1)}, bf16[512,2048]{1,0:T(8,128)(2,1)}, u32[]{:S(2)}, u32[]{:S(2)}) collective-permute-start(bf16[512,2048]{1,0:T(8,128)(2,1)} %add_convert_fusion.2.sa), channel_id=1, source_target_pairs={{0,2},{2,0},{1,3},{3,1},{4,6},{6,4},{5,7},{7,5}} | collective-permute-start | bytes 6291464 | tf_op jit(solution)/shard_map/ppermute | solution.py:418
  392.8 16.1 %slice-start = ((s8[8388608]{0:T(1024)(128)(4,1)}), s8[4194304]{0:T(1024)(128)(4,1)S(1)}, s32[]{:S(2)}) async-start(s8[8388608]{0:T(1024)(128)(4,1)} %bitcast.67), calls=%async_computation | async-start | bytes 8388608
  395.2 9.8 %copy-start.2 = (bf16[2,512,2048]{2,1,0:T(8,128)(2,1)S(1)}, bf16[2,512,2048]{2,1,0:T(8,128)(2,1)}, u32[]{:S(2)}) copy-start(bf16[2,512,2048]{2,1,0:T(8,128)(2,1)} %shard_map.147) | copy-start | bytes 12582916
  395.2 13.6 %slice-start.1 = ((s8[8388608]{0:T(1024)(128)(4,1)}), s8[4194304]{0:T(1024)(128)(4,1)S(1)}, s32[]{:S(2)}) async-start(s8[8388608]{0:T(1024)(128)(4,1)} %bitcast.67), calls=%async_computation.1 | async-start | bytes 8388608
  404.1 4.8 copy-start.1
  404.1 4.8 copy-start.8
  404.1 81.7 %collective-permute-start.20 = (bf16[512,2048]{1,0:T(8,128)(2,1)}, bf16[512,2048]{1,0:T(8,128)(2,1)}, u32[]{:S(2)}, u32[]{:S(2)}) collective-permute-start(bf16[512,2048]{1,0:T(8,128)(2,1)} %add_convert_fusion.1.sa), channel_id=1, source_target_pairs={{0,2},{2,0},{1,3},{3,1},{4,6},{6,4},{5,7},{7,5}} | collective-permute-start | bytes 6291464 | tf_op jit(solution)/shard_map/ppermute | solution.py:418
  441.3 8.6 %copy-start.13 = (f32[2048]{0:T(1024)S(1)}, f32[2048]{0:T(1024)}, u32[]{:S(2)}) copy-start(f32[2048]{0:T(1024)} %param.12) | copy-start | bytes 24580
  441.3 8.6 %copy-start.14 = (f32[2048]{0:T(1024)S(1)}, f32[2048]{0:T(1024)}, u32[]{:S(2)}) copy-start(f32[2048]{0:T(1024)} %param.11) | copy-start | bytes 24580
  441.3 8.6 %copy-start.16 = (f32[2048]{0:T(1024)S(1)}, f32[2048]{0:T(1024)}, u32[]{:S(2)}) copy-start(f32[2048]{0:T(1024)} %copy-done.15) | copy-start | bytes 24580
  449.9 44.3 %collective-permute-start.22 = (bf16[512,2048]{1,0:T(8,128)(2,1)}, bf16[512,2048]{1,0:T(8,128)(2,1)S(1)}, u32[]{:S(2)}, u32[]{:S(2)}) collective-permute-start(bf16[512,2048]{1,0:T(8,128)(2,1)} %get-tuple-element.140), channel_id=1, source_target_pairs={{0,1},{1,0},{2,3},{3,2},{4,5},{5,4},{6,7},{7,6}} | collective-permute-start | bytes 6291464 | tf_op jit(solution)/shard_map/ppermute | solution.py:415
  494.2 4.7 collective-permute-start.21
  494.2 1.4 copy-start.11

commit v2 on v1

--- a/solution.py
+++ b/solution.py
@@ -17,6 +17,7 @@
 TILE = 256
 MB = 2**20
 SAME = [(0, 1), (1, 0), (2, 3), (3, 2)]
+MESH = pl.DeviceIdType.MESH
 CROSS = [(0, 2), (2, 0), (1, 3), (3, 1)]
 
 
@@ -40,15 +41,22 @@
     return pl.CostEstimate(flops=int(flops), bytes_accessed=int(nbytes), transcendentals=0)
 
 
-def _fwd_kernel(*refs, t, hd, first):
-    qkv_ref = refs[0]
-    o_ref, ofull_ref, lse_ref, tr_ref = refs[1:] if first else refs[4:]
+def _fwd_kernel(*refs, hd, r0, r1, first):
+    if first:
+        qkv_ref, o_ref, lse_ref, tr_ref = refs
+        for i in range(r0 // BQ):
+            rows = slice(i * BQ, (i + 1) * BQ)
+            tr_ref[0, :, rows] = qkv_ref[rows, :].T
+    else:
+        qkv_ref, tr_ref, o_ref, lse_ref = refs
     c = LOG2E * hd**-0.5
-    for i in range(t // BQ):
+    for i in range(r0 // BQ, r1 // BQ):
         w = (i + 1) * BQ
         rows = slice(i * BQ, w)
+        loc = slice(i * BQ - r0, w - r0)
         blk = qkv_ref[rows, :]
-        tr_ref[0, :, rows] = blk.T
+        if first:
+            tr_ref[0, :, rows] = blk.T
         scores = []
         for h in range(2):
             q = blk[:, 3 * hd * h : 3 * hd * h + hd]
@@ -68,32 +76,28 @@
         for h in range(2):
             vt = slice(3 * hd * h + 2 * hd, 3 * hd * h + 3 * hd)
             outs.append((_dot_t(tr_ref[0, vt, :w], ps[h]) * st[2 * h + 1 : 2 * h + 2]).astype(bf))
-            lse_ref[0, h : h + 1, rows] = st[2 * h : 2 * h + 1]
-        o = jnp.concatenate(outs, 0).T
-        o_ref[rows, :] = o
-        ofull_ref[rows, :] = o
-
-
-def _attn_fwd(qkv, hd, start, npair, prev):
+            lse_ref[0, h : h + 1, loc] = st[2 * h : 2 * h + 1]
+        o_ref[loc, :] = jnp.concatenate(outs, 0).T
+
+
+def _attn_fwd(qkv, hd, chunk, b, tr):
     t, w = qkv.shape
-    total = w // (6 * hd)
-    full = [jax.ShapeDtypeStruct((t, total * 2 * hd), bf), jax.ShapeDtypeStruct((total, 2, t), f32), jax.ShapeDtypeStruct((total, 6 * hd, t), bf)]
-    return pl.pallas_call(
-        functools.partial(_fwd_kernel, t=t, hd=hd, first=prev is None),
+    npair = w // (6 * hd)
+    r0, r1 = chunk * b, (chunk + 1) * b
+    first = tr is None
+    trans = pl.BlockSpec((1, 6 * hd, r1), lambda p: (p, 0, 0))
+    res = pl.pallas_call(
+        functools.partial(_fwd_kernel, hd=hd, r0=r0, r1=r1, first=first),
         grid=(npair,),
-        in_specs=[pl.BlockSpec((t, 6 * hd), lambda p: (0, p + start))] + ([] if prev is None else [pl.BlockSpec(memory_space=pl.ANY)] * 3),
-        out_specs=[
-            pl.BlockSpec((t, 2 * hd), lambda p: (0, p)),
-            pl.BlockSpec((t, 2 * hd), lambda p: (0, p + start)),
-            pl.BlockSpec((1, 2, t), lambda p: (p + start, 0, 0)),
-            pl.BlockSpec((1, 6 * hd, t), lambda p: (p + start, 0, 0)),
-        ],
-        out_shape=[jax.ShapeDtypeStruct((t, npair * 2 * hd), bf)] + full,
-        input_output_aliases={} if prev is None else {1: 1, 2: 2, 3: 3},
+        in_specs=[pl.BlockSpec((r1, 6 * hd), lambda p: (0, p))] + ([] if first else [trans]),
+        out_specs=[pl.BlockSpec((b, 2 * hd), lambda p: (0, p)), pl.BlockSpec((1, 2, b), lambda p: (p, 0, 0))]
+        + ([trans] if first else []),
+        out_shape=[jax.ShapeDtypeStruct((b, npair * 2 * hd), bf), jax.ShapeDtypeStruct((npair, 2, b), f32)]
+        + ([jax.ShapeDtypeStruct((npair, 6 * hd, t), bf)] if first else []),
         compiler_params=_params(),
-        cost_estimate=_cost(npair * 9.5e9, npair * 2 * t * hd * 16),
-        name="attn_fwd",
-    )(qkv, *([] if prev is None else prev))
+        cost_estimate=_cost(npair * 2 * b * (r0 + r1) * 1200, npair * 2 * t * hd * 16),
+    )(qkv, *([] if first else [tr]))
+    return (*res, tr)[:3]
 
 
 def _bwd_kernel(*refs, hd, r0, r1, has_in, has_out):
@@ -103,8 +107,8 @@
     if has_in:
         acc_in, _ = refs[:2]
         refs = refs[2:]
-    own_ref, other_ref, full_ref = refs[:3]
-    refs = refs[3:]
+    pair_ref, full_ref = refs[:2]
+    refs = refs[2:]
     acc_out = None
     if has_out:
         acc_out = refs[0]
@@ -121,7 +125,7 @@
         blk = qkv_ref[loc, 0 : 4 * hd]
         do2 = do_ref[loc, :]
         do_t = do2.T
-        lse = lse_ref[0, :, rows].T
+        lse = lse_ref[0, :, loc].T
         prod = do2.astype(f32) * o_ref[loc, :].astype(f32)
         sd = []
         for h in range(2):
@@ -155,8 +159,8 @@
             outs += [(dq * sc).astype(bf), (g_t[kr, rows] * sc).astype(bf), g_t[vr, rows].astype(bf)]
         full_ref[loc, :] = jnp.concatenate(outs, 0).T
     half = (r1 - r0) // 2
-    own_ref[...] = full_ref[pl.ds(pl.multiple_of(ids[0] * half, half), half), :]
-    other_ref[...] = full_ref[pl.ds(pl.multiple_of((1 - ids[0]) * half, half), half), :]
+    pair_ref[0, 0] = full_ref[pl.ds(pl.multiple_of(ids[0] * half, half), half), :]
+    pair_ref[0, 1] = full_ref[pl.ds(pl.multiple_of((1 - ids[0]) * half, half), half), :]
     if has_out:
         acc_out[0] = g_t[:, :r0]
 
@@ -169,18 +173,18 @@
     in_specs = [
         pl.BlockSpec((b, 6 * hd), lambda p, s: (chunk, p)),
         pl.BlockSpec((1, 6 * hd, r1), lambda p, s: (p, 0, 0)),
-        pl.BlockSpec((b, 2 * hd), lambda p, s: (chunk, p)),
         pl.BlockSpec((b, 2 * hd), lambda p, s: (0, p)),
-        pl.BlockSpec((1, 2, t), lambda p, s: (p, 0, 0)),
+        pl.BlockSpec((b, 2 * hd), lambda p, s: (0, p)),
+        pl.BlockSpec((1, 2, b), lambda p, s: (p, 0, 0)),
     ]
     args = [qkv, tr, o, do, lse]
     alias = {}
     if has_in:
         in_specs += [pl.BlockSpec((1, 4 * hd, r1), lambda p, s: (p, 0, 0)), pl.BlockSpec(memory_space=pl.ANY)]
         args += [acc, full]
-        alias = {7: 2}
-    out_specs = [pl.BlockSpec((b // 2, 6 * hd), lambda p, s: (0, p))] * 2 + [pl.BlockSpec((b, 6 * hd), lambda p, s: (chunk, p))]
-    out_shape = [jax.ShapeDtypeStruct((b // 2, w), bf)] * 2 + [jax.ShapeDtypeStruct((t, w), bf)]
+        alias = {7: 1}
+    out_specs = [pl.BlockSpec((1, 2, b // 2, 6 * hd), lambda p, s: (0, 0, 0, p)), pl.BlockSpec((b, 6 * hd), lambda p, s: (chunk, p))]
+    out_shape = [jax.ShapeDtypeStruct((1, 2, b // 2, w), bf), jax.ShapeDtypeStruct((t, w), bf)]
     if has_out:
         out_specs.append(pl.BlockSpec((1, 4 * hd, r0), lambda p, s: (p, 0, 0)))
         out_shape.append(jax.ShapeDtypeStruct((npair, 4 * hd, r0), f32))
@@ -201,12 +205,11 @@
     )(ids, *args)
 
 
-def _h1_kernel(ids, x_ref, oa, ob, pa, pb, qa, qb, ra, rb, wa, wb, wc, wd, g_ref, xh_ref, rs_ref, own_ref, full_ref, acc):
+def _h1_kernel(ids, x_ref, oa, ob, oc, od, wa, wb, wc, wd, g_ref, xh_ref, rs_ref, own_ref, acc):
     def run(first, second):
-        acc[...] = sum(_dot(jnp.concatenate([u, v], 1), w[...]) for u, v, w in first + second)
-
-    near = [(oa[0, 0], ob[0, 0], wa), (pa[0, 0], pb[0, 0], wb)]
-    far = [(qa[0, 0], qb[0, 0], wc), (ra[0, 0], rb[0, 0], wd)]
+        acc[...] = sum(_dot(o[0], w[...]) for o, w in first + second)
+
+    near, far = [(oa, wa), (ob, wb)], [(oc, wc), (od, wd)]
 
     @pl.when(ids[1] == 0)
     def _():
@@ -224,79 +227,143 @@
     xh_ref[...] = xh
     rs_ref[...] = jnp.broadcast_to(rs, (rs.shape[0], 128))
     own_ref[...] = n2
-    full_ref[0] = n2
-
-
-def _h1(ids, chunk, x4, o_own, o_same, o_cross, o_diag, ws, g2):
+
+
+def _h1(ids, chunk, x4, os, ws, g2):
     _, _, r, d = x4.shape
-    own = lambda k: pl.BlockSpec((1, 1, TILE, k), lambda i, s: (chunk, s[0], i, 0))
-    flat = lambda k: pl.BlockSpec((TILE, k), lambda i, s: (i, 0))
+    k = os[0].shape[-1]
+    flat = lambda n: pl.BlockSpec((TILE, n), lambda i, s: (i, 0))
     const = lambda shape: pl.BlockSpec(shape, lambda i, s: (0, 0), pipeline_mode=pl.Buffered(1))
-    k = o_own[0].shape[-1]
     return pl.pallas_call(
         _h1_kernel,
         grid_spec=pltpu.PrefetchScalarGridSpec(
             num_scalar_prefetch=1,
             grid=(r // TILE,),
-            in_specs=[own(d)] + [own(k)] * 8
-            + [const((2 * k, d))] * 4
+            in_specs=[pl.BlockSpec((1, 1, TILE, d), lambda i, s: (chunk, s[0], i, 0))]
+            + [pl.BlockSpec((1, TILE, k), lambda i, s: (s[0], i, 0))] * 4
+            + [const((k, d))] * 4
             + [const((1, d))],
-            out_specs=[flat(d), flat(128), flat(d), pl.BlockSpec((1, TILE, d), lambda i, s: (s[0], i, 0))],
+            out_specs=[flat(d), flat(128), flat(d)],
             scratch_shapes=[pltpu.VMEM((TILE, d), f32)],
         ),
         out_shape=[
             jax.ShapeDtypeStruct((r, d), f32),
             jax.ShapeDtypeStruct((r, 128), f32),
             jax.ShapeDtypeStruct((r, d), bf),
-            jax.ShapeDtypeStruct((2, r, d), bf),
         ],
         compiler_params=_params(),
-        cost_estimate=_cost(2 * r * d * 8 * k, 20 * MB),
-    )(ids, x4, *o_own, *o_same, *o_cross, *o_diag, *ws, g2)
+        cost_estimate=_cost(8 * r * d * k, 20 * MB),
+    )(ids, x4, *os, *ws, g2)
 
 
 GC0 = 0.7978845608028654
 GC1 = 0.044715
 
 
-def _mlp_kernel(ids, n_ref, w_ref, dg_ref, *refs):
-    gl_ref, da_ref, own_ref, other_ref = refs[-4:]
-    sub = own_ref.shape[0]
-    for half in range(2):
-        rows = slice(half * sub, half * sub + sub)
-        a = _dot(n_ref[rows, :], w_ref[...])
+def _mlp_kernel(ids, own_n, other_n, w_ref, dg_ref, *refs):
+    gl_ref, da_ref, n_ref = refs[-3:]
+    sub = own_n.shape[0]
+    core = ids[0]
+    for half, at, src in ((0, core, own_n), (1, 1 - core, other_n)):
+        rows = pl.ds(pl.multiple_of(at * sub, sub), sub)
+        a = _dot(src[...], w_ref[...])
         a2 = a * a
         h = 0.5 + 0.5 * jnp.tanh(a * (GC0 + GC0 * GC1 * a2))
         gl_ref[rows, :] = (a * h).astype(bf)
-        slope = h + a * (2.0 * h * (1.0 - h)) * (GC0 + 3.0 * GC0 * GC1 * a2)
-        da_ref[rows, :] = (dg_ref[rows, :] * slope).astype(bf)
-    own_ref[...] = da_ref[pl.ds(pl.multiple_of(ids[0] * sub, sub), sub), :]
-    other_ref[...] = da_ref[pl.ds(pl.multiple_of((1 - ids[0]) * sub, sub), sub), :]
-
-
-def _mlp(ids, n2, w1, dg, chunk, prev, bn=512):
-    b, d = n2.shape
+        slope = h + a * (h * (1.0 - h)) * (2.0 * GC0 + 6.0 * GC0 * GC1 * a2)
+        da_ref[0, half] = (dg_ref[rows, :] * slope).astype(bf)
+
+    @pl.when(pl.program_id(0) == 0)
+    def _():
+        n_ref[0, 0] = own_n[...]
+        n_ref[0, 1] = other_n[...]
+
+
+def _mlp(ids, own, other, w1, dg, chunk, prev, bn=512):
+    r, d = own.shape
     t, f = dg.shape
-    spec = pl.BlockSpec((b, bn), lambda j, s: (chunk, j))
-    half = pl.BlockSpec((b // 2, bn), lambda j, s: (0, j))
+    spec = pl.BlockSpec((2 * r, bn), lambda j, s: (chunk, j))
+    pair = lambda k, f: pl.BlockSpec((1, 2, r, k), f)
+    rows = pl.BlockSpec((r, d), lambda j, s: (0, 0), pipeline_mode=pl.Buffered(1))
     return pl.pallas_call(
         _mlp_kernel,
         grid_spec=pltpu.PrefetchScalarGridSpec(
             num_scalar_prefetch=1,
             grid=(f // bn,),
-            in_specs=[
-                pl.BlockSpec((b, d), lambda j, s: (0, 0), pipeline_mode=pl.Buffered(1)),
-                pl.BlockSpec((d, bn), lambda j, s: (0, j)),
-                spec,
-            ]
+            in_specs=[rows, rows, pl.BlockSpec((d, bn), lambda j, s: (0, j)), spec]
             + [pl.BlockSpec(memory_space=pl.ANY)] * len(prev),
-            out_specs=[spec, spec, half, half],
+            out_specs=[spec, pair(bn, lambda j, s: (chunk, 0, 0, j)), pair(d, lambda j, s: (chunk, 0, 0, 0))],
         ),
-        out_shape=[jax.ShapeDtypeStruct((t, f), bf)] * 2 + [jax.ShapeDtypeStruct((b // 2, f), bf)] * 2,
-        input_output_aliases={4: 0, 5: 1} if prev else {},
+        out_shape=[
+            jax.ShapeDtypeStruct((t, f), bf),
+            jax.ShapeDtypeStruct((NB, 2, r, f), bf),
+            jax.ShapeDtypeStruct((NB, 2, r, d), bf),
+        ],
+        input_output_aliases={5: 0, 6: 1, 7: 2} if prev else {},
         compiler_params=_params(),
-        cost_estimate=_cost(2 * b * d * f * 1.3, 2 * b * f * 8),
-    )(ids, n2, w1, dg, *prev)
+        cost_estimate=_cost(4 * r * d * f * 1.3, 4 * r * f * 8),
+    )(ids, own, other, w1, dg, *prev)
+
+
+def _partial_kernel(v_ref, w_ref, out_ref, sent, got, send_sem, recv_sem, *, nt):
+    j = pl.program_id(0)
+    me = lax.axis_index("tp")
+    peer = {"tp": me + 1 - 2 * lax.rem(me, 2)}
+
+    def copy(i):
+        return pltpu.make_async_remote_copy(
+            src_ref=sent.at[i], dst_ref=got.at[i], send_sem=send_sem.at[i], recv_sem=recv_sem.at[i],
+            device_id=peer, device_id_type=MESH,
+        )
+
+    @pl.when(j == 0)
+    def _():
+        barrier = pltpu.get_barrier_semaphore()
+        pl.semaphore_signal(barrier, inc=1, device_id=peer, device_id_type=MESH)
+        pl.semaphore_wait(barrier, 1)
+
+    @pl.when((j >= 1) & (j <= nt))
+    def _():
+        copy(j - 1).start()
+
+    @pl.when(j < nt)
+    def _():
+        sent[j] = _dot_t(v_ref[0, 0], w_ref[...]).astype(bf)
+
+    @pl.when(j >= nt)
+    def _():
+        p = _dot_t(v_ref[0, 0], w_ref[...])
+        copy(j - nt).wait_recv()
+        out_ref[...] = (p + got[j - nt].astype(f32)).astype(bf)
+
+    @pl.when(j == 2 * nt - 1)
+    def _():
+        for i in range(nt):
+            copy(i).wait_send()
+
+
+def _partial(v4, chunk, w, cid, nt):
+    _, _, r, k = v4.shape
+    n = w.shape[0]
+    bn = n // nt
+    return pl.pallas_call(
+        functools.partial(_partial_kernel, nt=nt),
+        grid=(2 * nt,),
+        in_specs=[
+            pl.BlockSpec((1, 1, r, k), lambda j: (chunk, 1 - j // nt, 0, 0)),
+            pl.BlockSpec((bn, k), lambda j: (lax.rem(j, nt), 0)),
+        ],
+        out_specs=pl.BlockSpec((r, bn), lambda j: (0, jnp.maximum(j - nt, 0))),
+        out_shape=jax.ShapeDtypeStruct((r, n), bf),
+        scratch_shapes=[
+            pltpu.VMEM((nt, r, bn), bf),
+            pltpu.VMEM((nt, r, bn), bf),
+            pltpu.SemaphoreType.DMA((nt,)),
+            pltpu.SemaphoreType.DMA((nt,)),
+        ],
+        compiler_params=pltpu.CompilerParams(vmem_limit_bytes=60 * MB, collective_id=cid, has_side_effects=True),
+        cost_estimate=_cost(4 * r * k * n, 6 * r * k + 2 * n * k),
+    )(v4, w)
 
 
 def _place_kernel(ids, v_ref, _, buf_ref):
@@ -315,7 +382,7 @@
         ),
         out_shape=jax.ShapeDtypeStruct(buf.shape, buf.dtype),
         input_output_aliases={2: 0},
-        compiler_params=_params(),
+        compiler_params=_params(32),
         cost_estimate=_cost(r * d * 1000, 2 * r * d * 2),
     )(ids, v, buf)
 
@@ -336,7 +403,7 @@
         ),
         out_shape=jax.ShapeDtypeStruct(buf.shape, buf.dtype),
         input_output_aliases={2: 0},
-        compiler_params=_params(),
+        compiler_params=_params(32),
         cost_estimate=_cost(r * d * 1000, 2 * r * d * 2),
     )(ids, v, buf)
 
@@ -382,7 +449,7 @@
         ),
         out_shape=outs,
         input_output_aliases=alias or {},
-        compiler_params=_params(),
+        compiler_params=_params(32),
         cost_estimate=_cost(r * 2048 * 6000, r * 2048 * 16),
     )(ids, *args)
 
@@ -432,46 +499,36 @@
         n1 = ((xf - mu1[:, None]) * rs1[:, None] * g1.astype(f32)).astype(bf)
         qkv = did(_dot(n1, wqkv).astype(bf))
 
-        o_own, o_same, o_cross, o_diag = [], [], [], []
-        npair = hl // 4
-        prev = None
-        for s in range(2):
-            o, *prev = _attn_fwd(tie(qkv), hd, s * npair, npair, prev)
-            did(o)
-            oc = cross(o)
-            o_own.append(split(o))
-            o_cross.append(split(oc))
-            o_same.append(split(same(o)))
-            o_diag.append(split(same(oc)))
-        o_all, lse, qkv_t = prev
+        pair_rows = lambda v: v.reshape(2, r, v.shape[-1])
+        o, lse, os = [None] * NB, [None] * NB, [None] * NB
+        qkv_t = None
+        for k in chunks:
+            o[k], lse[k], qkv_t = _attn_fwd(tie(qkv), hd, k, b, qkv_t)
+            did(o[k])
+            o_cross = cross(o[k])
+            o_same, o_diag = same(o[k]), same(o_cross)
+            os[k] = [pair_rows(v) for v in (o[k], o_same, o_cross, o_diag)]
 
         dg = did(_dot_t(tie(dy), w2))
 
         x4, dy4 = split(x), split(dy)
         xh2, rs2, n2, others = [None] * NB, [None] * NB, [None] * NB, [None] * NB
         for k in chunks:
-            xh2[k], rs2[k], own, n2[k] = _h1(
-                ids, k, tie(x4), o_own, o_same, o_cross, o_diag, (wo2, wo_same, wo_cross, wo_diag), g2[None]
+            xh2[k], rs2[k], n2[k] = _h1(
+                ids, k, tie(x4), os[k], (wo2, wo_same, wo_cross, wo_diag), g2[None]
             )
-            did(own)
-            others[k] = same(own)
-
-        sums, n2f = [None] * NB, [None] * NB
-
-        def place_n2(k):
-            n2f[k] = did(_place(ids, tie(n2[k]), others[k])).reshape(b, d)
+            did(n2[k])
+            others[k] = same(n2[k])
+
+        sums = [None] * NB
 
         def mlp(k, prev):
-            res = _mlp(ids, tie(n2f[k]), w1, dg, k, prev)
+            res = _mlp(ids, tie(n2[k]), others[k], w1, dg, k, prev)
             did(res[1])
             return res
 
-        def partial_other(v, w):
-            p = did(_dot_t(tie(v), w).astype(bf))
-            return same(p)
-
-        def partial_own(v, w, recv):
-            s_own = did((_dot_t(tie(v), w) + recv.astype(f32)).astype(bf))
+        def partial(v4, k, w, cid):
+            s_own = did(_partial(tie(v4), k, w, cid, 2))
             return s_own, cross(s_own)
 
         def grad(u, v, add=None, keep=False):
@@ -485,7 +542,7 @@
             dh[k], own, dhb[k] = _lnb(
                 _lnb2_kernel, ids, k, (tie(sums[k][0]), sums[k][1], xh2[k], rs2[k], dy4, g2[None]),
                 ("flat", "flat", "flat", "flat", "own", "gain"),
-                (sds((r, d), f32), sds((r, d), bf), sds((2, r, d), bf)), ("flat", "flat", "pair"),
+                (pltpu.HBM((r, d), f32), sds((r, d), bf), sds((2, r, d), bf)), ("flat", "flat", "pair"),
             )
             did(own)
             return same(own)
@@ -493,7 +550,7 @@
         def attention(k, other, acc, full):
             dhb[k] = did(_place(ids, tie(dhb[k]), other)).reshape(b, d)
             do = did(_dot_t(tie(dhb[k]), wo2).astype(bf))
-            res = _attn_bwd(ids, qkv, qkv_t, o_all, do, lse, acc, full, k, b, hd)
+            res = _attn_bwd(ids, qkv, qkv_t, o[k], do, lse[k], acc, full, k, b, hd)
             did(res[0])
             return res
 
@@ -507,30 +564,23 @@
             did(own)
             return same(own), dx
 
-        place_n2(1)
-        *gd, da_own, da_other = mlp(1, ())
-        recv = partial_other(da_other, w1)
-        place_n2(0)
-        sums[1] = partial_own(da_own, w1, recv)
-        gl, da, da_own, da_other = mlp(0, gd)
-        recv = partial_other(da_other, w1)
+        gd = mlp(1, ())
+        sums[1] = partial(gd[1], 1, w1, 1)
+        gl, da, n2_all = mlp(0, gd)
         dw2 = grad(gl, dy)
         other = norm2(1)
-        sums[0] = partial_own(da_own, w1, recv)
+        sums[0] = partial(da, 0, w1, 2)
 
         mu4, rs4 = mu1.reshape(NB, 2, 1, r), rs1.reshape(NB, 2, 1, r)
-        o3 = o_all.reshape(NB, b, -1)
-
-        own1, oth1, full, acc = attention(1, other, None, None)
-        recv = partial_other(oth1, wqkv)
+
+        pair, full, acc = attention(1, other, None, None)
+        pair1 = partial(pair, 0, wqkv, 3)
         other = norm2(0)
-        pair1 = partial_own(own1, wqkv, recv)
-        own0, oth0, full = attention(0, other, acc, full)
-        recv = partial_other(oth0, wqkv)
-        dwo = grad(o3[1], dhb[1], keep=True)
-        pair0 = partial_own(own0, wqkv, recv)
-        dwo = grad(o3[0], dhb[0], dwo).reshape(hl, hd, d)
-        dw1 = grad(jnp.concatenate(n2f, 0), da)
+        dwo = grad(o[1], dhb[1], keep=True)
+        pair, full = attention(0, other, acc, full)
+        pair0 = partial(pair, 0, wqkv, 4)
+        dwo = grad(o[0], dhb[0], dwo).reshape(hl, hd, d)
+        dw1 = grad(n2_all.reshape(t, d), da.reshape(t, -1))
         other1, dx = norm1(1, pair1, None)
         dwqkv = grad(n1, full)
         other0, dx = norm1(0, pair0, dx)

time: 511 us -> 432 us (0.85)
  matrix products: 194 us -> 130 us
  waiting for transfers between devices: 71.3 us -> 23.1 us
  Pallas kernels: 218 us -> 245 us
  local copies, waits for them, and re-layouts: 4.53 us -> 11.5 us
    dot_general x11 -> x3, matrix products: 104 us -> 31.5 us  [_dot_t(): lax.dot_general(a, b, (((1,), (1,)), ((), ())), preferred_element_type=f32)]
    ppermute x7, waiting for transfers between devices: 69.6 us -> 14.4 us  [cross(): return lax.ppermute(v, 'tp', CROSS)]
    pallas_call x2 -> x6, Pallas kernels: 36.9 us -> 91.4 us  [the longest x4 55.1 us: _partial(): pl.pallas_call(functools.partial(_partial_kernel, nt=nt), grid=(2 * nt,),...]
    pallas_call x4 -> x2, Pallas kernels: 13.8 us -> 1.87 us  [_place(): pl.pallas_call(_place_kernel, grid_spec=pltpu.PrefetchScalarGridSpec(num_...]
    pallas_call x4, Pallas kernels: 35.6 us -> 23.7 us  [_lnb(): pl.pallas_call(kernel, grid_spec=pltpu.PrefetchScalarGridSpec(num_scalar_...]
    dot_general x6, matrix products: 90.8 us -> 98.6 us  [_dot(): return jnp.dot(a, b, preferred_element_type=f32)]
    unnamed x48 -> x70, local copies, waits for them, and re-layouts: 3.33 us -> 10.9 us
    ppermute x16 -> x12, waiting for transfers between devices: 1.68 us -> 8.67 us  [same(): return lax.ppermute(v, 'tp', SAME)]
  transfers between devices with their start and end apart: 23 -> 19, of which waited for: 6 -> 5; matrix products, arithmetic and copies ran while one was open for 35% -> 31% of each run, Pallas kernels for 36% -> 54%
where the time goes in v2:
time: 432 us; the launch traced here: 424 us
  Pallas kernels  245 us (57%)
  matrix products  130 us (30%)
  waiting for transfers between devices  23.1 us (5%)
  local copies, waits for them, and re-layouts  11.5 us (3%)
  starting transfers between devices  10.8 us (2%)
    dot_general x6, matrix products, _dot(): return jnp.dot(a, b, preferred_element_type=f32)  98.6 us
    pallas_call x2, Pallas kernels, _attn_bwd(): pl.pallas_call(functools.partial(_bwd_kernel, hd=hd, r0=r0, r1=r1, has_in...  57.9 us
    pallas_call x4, Pallas kernels, _partial(): pl.pallas_call(functools.partial(_partial_kernel, nt=nt), grid=(2 * nt,),...  55.1 us
    pallas_call x2, Pallas kernels, _mlp(): pl.pallas_call(_mlp_kernel, grid_spec=pltpu.PrefetchScalarGridSpec(num_sc...  40.8 us
    pallas_call x2, Pallas kernels, _attn_fwd(): pl.pallas_call(functools.partial(_fwd_kernel, hd=hd, r0=r0, r1=r1, first=...  36.3 us
    dot_general x3, matrix products, _dot_t(): lax.dot_general(a, b, (((1,), (1,)), ((), ())), preferred_element_type=f32)  31.5 us
    pallas_call x2, Pallas kernels, _h1(): pl.pallas_call(_h1_kernel, grid_spec=pltpu.PrefetchScalarGridSpec(num_sca...  25.9 us
    pallas_call x4, Pallas kernels, _lnb(): pl.pallas_call(kernel, grid_spec=pltpu.PrefetchScalarGridSpec(num_scalar_...  23.7 us
  transfers between devices with their start and end apart: 19, of which 5 were waited for; matrix products, arithmetic and copies ran while one was open for 31% of the time, Pallas kernels for 54%

profile of v2, /device:TPU:0, one launch (start us, length us, event | category | flops | bytes accessed | tf_op | source)
XLA Modules:
  0.0 423.7 jit_solution(18344588238534020261)
XLA Ops:
  0.6 3.3 collective-permute-start.4
  4.0 0.7 convert_element_type.31
  4.7 0.6 copy-done.30
  5.2 19.0 %convolution_convert_fusion.2.refs_0_.refs_1_ = bf16[2048,1536]{1,0:T(8,128)(2,1)} fusion(bf16[2048,1536]{1,0:T(8,128)(2,1)} %w_ref.11, bf16[2048,2048]{1,0:T(8,128)(2,1)} %param.10, f32[2048]{0:T(1024)S(1)} %convert_element_type.31, f32[2048]{0:T(1024)} %param.12, f32[2048]{0:T(1024)} %param.11), kind=kOutput, calls=%fused_computation.3 | convolution fusion | flops 12909019136 | bytes 20996096 | tf_op jit(solution)/shard_map/dot_general | solution.py:25
  24.3 23.9 %shard_map.137 = (bf16[1024,512]{1,0:T(8,128)(2,1)}, f32[4,2,1024]{2,1,0:T(2,128)}, bf16[4,384,2048]{2,1,0:T(8,128)(2,1)}) custom-call(bf16[2048,1536]{1,0:T(8,128)(2,1)} %convolution_convert_fusion.2.refs_0_.refs_1_), custom_call_target="tpu_custom_call" | custom-call | flops 30198988800 | bytes 16777216 | tf_op jit(solution)/shard_map/pallas_call | solution.py:89
  48.7 12.4 %shard_map.138 = (bf16[1024,512]{1,0:T(8,128)(2,1)}, f32[4,2,1024]{2,1,0:T(2,128)}) custom-call(bf16[2048,1536]{1,0:T(8,128)(2,1)} %convolution_convert_fusion.2.refs_0_.refs_1_, bf16[4,384,2048]{2,1,0:T(8,128)(2,1)} %get-tuple-element.60.refs_1_.refs_2_), custom_call_target="tpu_custom_call" | custom-call | flops 10066329600 | bytes 16777216 | tf_op jit(solution)/shard_map/pallas_call | solution.py:89
  61.1 2.0 collective-permute-start.7
  63.1 11.3 %collective-permute-done.1 = bf16[1024,512]{1,0:T(8,128)(2,1)S(1)} collective-permute-done((bf16[1024,512]{1,0:T(8,128)(2,1)}, bf16[1024,512]{1,0:T(8,128)(2,1)S(1)}, u32[]{:S(2)}, u32[]{:S(2)}) %collective-permute-start.1) | collective-permute-done | bytes 1048608 | tf_op jit(solution)/shard_map/ppermute | solution.py:485
  74.4 0.5 collective-permute-start.5
  74.9 24.8 %fusion.dg_ref = f32[2048,2048]{1,0:T(8,128)} fusion(bf16[2048,2048]{1,0:T(8,128)(2,1)} %param.15, bf16[2048,2048]{1,0:T(8,128)(2,1)} %param.19), kind=kOutput, calls=%fused_computation.9 | convolution fusion | flops 17179869184 | bytes 33554432 | tf_op jit(solution)/shard_map/dot_general | solution.py:29
  99.7 0.6 broadcast_in_dim.4.g_ref
  100.3 0.6 pad_add_fusion.ids.refs_0_
  101.0 12.9 %shard_map.139 = (f32[512,2048]{1,0:T(8,128)}, f32[512,128]{1,0:T(8,128)}, bf16[512,2048]{1,0:T(8,128)(2,1)}) custom-call(s32[2]{0:T(128)} %pad_add_fusion.ids.refs_0_, bf16[2,2,512,2048]{3,2,1,0:T(8,128)(2,1)} %bitcast.37, bf16[2,512,512]{2,1,0:T(8,128)(2,1)} %bitcast.60, bf16[2,512,512]{2,1,0:T(8,128)(2,1)} %bitcast.4.ob, bf16[2,512,512]{2,1,0:T(8,128)(2,1)} %bitcast.63, ...), custom_call_target="tpu_custom_call" | custom-call | flops 4294967296 | bytes 20971520 | tf_op jit(solution)/shard_map/pallas_call | solution.py:237
  114.5 5.3 %collective-permute-done.6 = bf16[1024,512]{1,0:T(8,128)(2,1)S(1)} collective-permute-done((bf16[1024,512]{1,0:T(8,128)(2,1)S(1)}, bf16[1024,512]{1,0:T(8,128)(2,1)S(1)}, u32[]{:S(2)}, u32[]{:S(2)}) %collective-permute-start.6) | collective-permute-done | bytes 1048608 | tf_op jit(solution)/shard_map/ppermute | solution.py:482
  119.8 1.5 collective-permute-done.8
  121.3 1.0 copy-done.28
  122.3 13.0 %shard_map.140 = (f32[512,2048]{1,0:T(8,128)}, f32[512,128]{1,0:T(8,128)}, bf16[512,2048]{1,0:T(8,128)(2,1)}) custom-call(s32[2]{0:T(128)} %pad_add_fusion.ids.refs_0_, bf16[2,2,512,2048]{3,2,1,0:T(8,128)(2,1)} %bitcast.38, bf16[2,512,512]{2,1,0:T(8,128)(2,1)} %bitcast.61, bf16[2,512,512]{2,1,0:T(8,128)(2,1)} %bitcast.64, bf16[2,512,512]{2,1,0:T(8,128)(2,1)} %bitcast.10.oc, ...), custom_call_target="tpu_custom_call" | custom-call | flops 4294967296 | bytes 20971520 | tf_op jit(solution)/shard_map/pallas_call | solution.py:237
  135.4 20.3 %shard_map.141 = (bf16[2048,2048]{1,0:T(8,128)(2,1)}, bf16[2,2,512,2048]{3,2,1,0:T(8,128)(2,1)}, bf16[2,2,512,2048]{3,2,1,0:T(8,128)(2,1)}) custom-call(s32[2]{0:T(128)} %pad_add_fusion.ids.refs_0_, bf16[512,2048]{1,0:T(8,128)(2,1)} %get-tuple-element.69.own_n, bf16[512,2048]{1,0:T(8,128)(2,1)} %collective-permute-done.9.other_n, bf16[2048,2048]{1,0:T(8,128)(2,1)} %w_ref.9, ...), custom_call_target="tpu_custom_call" | custom-call | flops 11166914560 | bytes 33554432 | tf_op jit(solution)/shard_map/pallas_call | solution.py:288
  155.7 15.1 %shard_map.142.sa = bf16[512,2048]{1,0:T(8,128)(2,1)} custom-call(bf16[2,2,512,2048]{3,2,1,0:T(8,128)(2,1)} %get-tuple-element.71.v_ref.refs_1_, bf16[2048,2048]{1,0:T(8,128)(2,1)} %w_ref.9), custom_call_target="tpu_custom_call" | custom-call | flops 8589934592 | bytes 14680064 | tf_op jit(solution)/shard_map/pallas_call | solution.py:349
  171.3 20.5 %shard_map.143 = (bf16[2048,2048]{1,0:T(8,128)(2,1)}, bf16[2,2,512,2048]{3,2,1,0:T(8,128)(2,1)}, bf16[2,2,512,2048]{3,2,1,0:T(8,128)(2,1)}) custom-call(s32[2]{0:T(128)} %pad_add_fusion.ids.refs_0_, bf16[512,2048]{1,0:T(8,128)(2,1)} %get-tuple-element.72.own_n, ...), custom_call_target="tpu_custom_call", output_to_operand_aliasing={{0}: (5, {}), {1}: (6, {}), {2}: (7, {})} | custom-call | flops 11166914560 | bytes 33554432 | tf_op jit(solution)/shard_map/pallas_call | solution.py:288
  191.8 23.8 %convolution_convert_fusion.1 = bf16[2048,2048]{1,0:T(8,128)(2,1)} fusion(bf16[2048,2048]{1,0:T(8,128)(2,1)} %get-tuple-element.76, bf16[2048,2048]{1,0:T(8,128)(2,1)} %param.15), kind=kOutput, calls=%fused_computation.2 | convolution fusion | flops 17184063488 | bytes 25165824 | tf_op jit(solution)/shard_map/dot_general | solution.py:25
  215.6 3.1 collective-permute-done.11.sb
  218.8 6.3 %shard_map.144 = (f32[512,2048]{1,0:T(8,128)}, bf16[512,2048]{1,0:T(8,128)(2,1)}, bf16[2,512,2048]{2,1,0:T(8,128)(2,1)S(1)}) custom-call(s32[2]{0:T(128)S(1)} %copy-done.8, bf16[512,2048]{1,0:T(8,128)(2,1)S(1)} %copy-done.16, bf16[512,2048]{1,0:T(8,128)(2,1)S(1)} %collective-permute-done.11.sb, f32[512,2048]{1,0:T(8,128)S(1)} %copy-done.14, ...), custom_call_target="tpu_custom_call" | custom-call | flops 6291456000 | bytes 16777216 | tf_op jit(solution)/shard_map/pallas_call | solution.py:442
  225.1 2.0 copy-done
  227.1 15.2 %shard_map.145.sa = bf16[512,2048]{1,0:T(8,128)(2,1)} custom-call(bf16[2,2,512,2048]{3,2,1,0:T(8,128)(2,1)} %get-tuple-element.82.v_ref, bf16[2048,2048]{1,0:T(8,128)(2,1)} %w_ref.9), custom_call_target="tpu_custom_call" | custom-call | flops 8589934592 | bytes 14680064 | tf_op jit(solution)/shard_map/pallas_call | solution.py:349
  242.8 2.2 copy-done.1
  245.0 1.1 shard_map.146
  246.6 3.3 convolution_convert_fusion.5.refs_4_
  249.9 38.8 %shard_map.147 = (bf16[1,2,512,1536]{3,2,1,0:T(8,128)(2,1)}, bf16[2048,1536]{1,0:T(8,128)(2,1)}, f32[4,256,1024]{2,1,0:T(8,128)}) custom-call(s32[2]{0:T(128)} %pad_add_fusion.ids.refs_0_, bf16[2048,1536]{1,0:T(8,128)(2,1)} %convolution_convert_fusion.2.refs_0_.refs_1_, bf16[4,384,2048]{2,1,0:T(8,128)(2,1)} %get-tuple-element.60.refs_1_.refs_2_, ...), custom_call_target="tpu_custom_call" | custom-call | flops 37748736000 | bytes 9437184 | tf_op jit(solution)/shard_map/pallas_call | solution.py:192
  288.8 12.3 %shard_map.148.sa = bf16[512,2048]{1,0:T(8,128)(2,1)} custom-call(bf16[1,2,512,1536]{3,2,1,0:T(8,128)(2,1)} %get-tuple-element.87.v_ref, bf16[2048,1536]{1,0:T(8,128)(2,1)} %w_ref.11), custom_call_target="tpu_custom_call" | custom-call | flops 6442450944 | bytes 11010048 | tf_op jit(solution)/shard_map/pallas_call | solution.py:349
  301.1 2.2 copy-done.13
  303.3 1.6 copy-done.15
  304.9 6.6 %shard_map.149 = (f32[512,2048]{1,0:T(8,128)}, bf16[512,2048]{1,0:T(8,128)(2,1)S(1)}, bf16[2,512,2048]{2,1,0:T(8,128)(2,1)S(1)}) custom-call(s32[2]{0:T(128)S(1)} %copy-done.9, bf16[512,2048]{1,0:T(8,128)(2,1)S(1)} %copy-done.15, bf16[512,2048]{1,0:T(8,128)(2,1)} %collective-permute-done.13.sb, f32[512,2048]{1,0:T(8,128)S(1)} %copy-done.13, ...), custom_call_target="tpu_custom_call" | custom-call | flops 6291456000 | bytes 16777216 | tf_op jit(solution)/shard_map/pallas_call | solution.py:442
  311.9 1.7 collective-permute-start.15
  313.6 4.3 %fusion.1 = f32[512,2048]{1,0:T(8,128)} fusion(bf16[1024,512]{1,0:T(8,128)(2,1)S(1)} %copy-done.23, bf16[1024,2048]{1,0:T(8,128)(2,1)S(1)} %bitcast.44), kind=kOutput, calls=%fused_computation.10 | convolution fusion | flops 2147483648 | bytes 9437184 | tf_op jit(solution)/shard_map/dot_general | solution.py:25
  317.9 0.7 shard_map.150
  318.7 0.8 copy-done.22
  319.5 3.3 convolution_convert_fusion.4.refs_4_
  322.9 19.0 %shard_map.151 = (bf16[1,2,512,1536]{3,2,1,0:T(8,128)(2,1)}, bf16[2048,1536]{1,0:T(8,128)(2,1)}) custom-call(s32[2]{0:T(128)} %pad_add_fusion.ids.refs_0_, bf16[2048,1536]{1,0:T(8,128)(2,1)} %convolution_convert_fusion.2.refs_0_.refs_1_, bf16[4,384,2048]{2,1,0:T(8,128)(2,1)} %get-tuple-element.60.refs_1_.refs_2_, ...), custom_call_target="tpu_custom_call", output_to_operand_aliasing={{1}: (7, {})} | custom-call | flops 12582912000 | bytes 9437184 | tf_op jit(solution)/shard_map/pallas_call | solution.py:192
  341.9 12.4 %shard_map.152.sa = bf16[512,2048]{1,0:T(8,128)(2,1)} custom-call(bf16[1,2,512,1536]{3,2,1,0:T(8,128)(2,1)} %get-tuple-element.99.v_ref, bf16[2048,1536]{1,0:T(8,128)(2,1)} %w_ref.11), custom_call_target="tpu_custom_call" | custom-call | flops 6442450944 | bytes 11010048 | tf_op jit(solution)/shard_map/pallas_call | solution.py:349
  354.7 7.3 %add_convert_fusion = bf16[512,2048]{1,0:T(8,128)(2,1)} fusion(f32[512,2048]{1,0:T(8,128)} %fusion.1, bf16[1024,512]{1,0:T(8,128)(2,1)S(1)} %copy-done.25, bf16[1024,2048]{1,0:T(8,128)(2,1)} %bitcast.46), kind=kOutput, calls=%fused_computation.5 | convolution fusion | flops 2149580800 | bytes 11534336 | tf_op jit(solution)/shard_map/dot_general | solution.py:25
  362.1 23.8 %convolution_convert_fusion = bf16[2048,2048]{1,0:T(8,128)(2,1)} fusion(bf16[2048,2048]{1,0:T(8,128)(2,1)} %bitcast.53, bf16[2048,2048]{1,0:T(8,128)(2,1)} %bitcast.52), kind=kOutput, calls=%fused_computation.1 | convolution fusion | flops 17184063488 | bytes 25165824 | tf_op jit(solution)/shard_map/dot_general | solution.py:25
  385.9 6.3 %shard_map.153 = (bf16[512,2048]{1,0:T(8,128)(2,1)}, bf16[2,2,512,2048]{3,2,1,0:T(8,128)(2,1)}) custom-call(s32[2]{0:T(128)S(1)} %copy-done.10, bf16[512,2048]{1,0:T(8,128)(2,1)} %shard_map.148.sa, bf16[512,2048]{1,0:T(8,128)(2,1)S(1)} %collective-permute-done.15.sb, bf16[2,2,512,2048]{3,2,1,0:T(8,128)(2,1)S(1)} %bitcast.41, f32[2,2,1,512]{3,2,1,0:T(1,128)S(1)} %bitcast.49, ...), custom_call_target="tpu_custom_call" | custom-call | flops 6291456000 | bytes 16777216 | tf_op jit(solution)/shard_map/pallas_call | solution.py:442
  392.4 20.3 %convolution_convert_fusion.3 = bf16[2048,1536]{1,0:T(8,128)(2,1)} fusion(bf16[2048,1536]{1,0:T(8,128)(2,1)} %get-tuple-element.107, bf16[2048,2048]{1,0:T(8,128)(2,1)S(1)} %bitcast.40, f32[2048]{0:T(1024)S(1)} %copy-done.31, f32[2048]{0:T(1024)S(1)} %copy-done.11, f32[2048]{0:T(1024)S(1)} %copy-done.12), kind=kOutput, calls=%fused_computation.4 | convolution fusion | flops 12909019136 | bytes 20996096 | tf_op jit(solution)/shard_map/dot_general | solution.py:25
  412.7 4.4 %shard_map.154 = (bf16[512,2048]{1,0:T(8,128)(2,1)S(1)}, bf16[2,2,512,2048]{3,2,1,0:T(8,128)(2,1)}) custom-call(s32[2]{0:T(128)S(1)} %copy-done.10, bf16[512,2048]{1,0:T(8,128)(2,1)S(1)} %copy-done.6, bf16[512,2048]{1,0:T(8,128)(2,1)S(1)} %collective-permute-done.16.sb, bf16[2,2,512,2048]{3,2,1,0:T(8,128)(2,1)S(1)} %bitcast.42, ...), custom_call_target="tpu_custom_call", output_to_operand_aliasing={{1}: (8, {})} | custom-call | flops 6291456000 | bytes 16777216 | tf_op jit(solution)/shard_map/pallas_call | solution.py:442
  417.5 1.9 shard_map.155._
  419.5 1.8 collective-permute-done.17.v_ref
  421.3 1.9 shard_map.156
  (94 shorter events, 3.9 us)
Async XLA Ops:
  0.6 73.8 %collective-permute-start.4 = (bf16[512,2048]{1,0:T(8,128)(2,1)}, bf16[512,2048]{1,0:T(8,128)(2,1)}, u32[]{:S(2)}, u32[]{:S(2)}) collective-permute-start(bf16[512,2048]{1,0:T(8,128)(2,1)} %bitcast.54), channel_id=1, source_target_pairs={{0,2},{2,0},{1,3},{3,1},{4,6},{6,4},{5,7},{7,5}} | collective-permute-start | bytes 6291464 | tf_op jit(solution)/shard_map/ppermute | solution.py:485
  24.3 23.9 %copy-start.20 = (bf16[8,64,2048]{2,1,0:T(8,128)(2,1)S(1)}, bf16[8,64,2048]{2,1,0:T(8,128)(2,1)}, u32[]{:S(2)}) copy-start(bf16[8,64,2048]{2,1,0:T(8,128)(2,1)} %param.17) | copy-start | bytes 6291460
  48.1 26.2 %collective-permute-start.1 = (bf16[1024,512]{1,0:T(8,128)(2,1)}, bf16[1024,512]{1,0:T(8,128)(2,1)S(1)}, u32[]{:S(2)}, u32[]{:S(2)}) collective-permute-start(bf16[1024,512]{1,0:T(8,128)(2,1)} %get-tuple-element.61.refs_3_), channel_id=1, source_target_pairs={{0,2},{2,0},{1,3},{3,1},{4,6},{6,4},{5,7},{7,5}} | collective-permute-start | bytes 3145736 | tf_op jit(solution)/shard_map/ppermute | solution.py:485
  48.2 52.8 %collective-permute-start = (bf16[1024,512]{1,0:T(8,128)(2,1)}, bf16[1024,512]{1,0:T(8,128)(2,1)}, u32[]{:S(2)}, u32[]{:S(2)}) collective-permute-start(bf16[1024,512]{1,0:T(8,128)(2,1)} %get-tuple-element.61.refs_3_), channel_id=1, source_target_pairs={{0,1},{1,0},{2,3},{3,2},{4,5},{5,4},{6,7},{7,6}} | collective-permute-start | bytes 3145736 | tf_op jit(solution)/shard_map/ppermute | solution.py:482
  48.2 52.8 %collective-permute-start.3 = (bf16[512,2048]{1,0:T(8,128)(2,1)S(1)}, bf16[512,2048]{1,0:T(8,128)(2,1)}, u32[]{:S(2)}, u32[]{:S(2)}) collective-permute-start(bf16[512,2048]{1,0:T(8,128)(2,1)S(1)} %bitcast.57), channel_id=1, source_target_pairs={{0,1},{1,0},{2,3},{3,2},{4,5},{5,4},{6,7},{7,6}} | collective-permute-start | bytes 6291464 | tf_op jit(solution)/shard_map/ppermute | solution.py:482
  61.1 38.7 %copy-start.32 = (bf16[2048]{0:T(1024)(128)(2,1)S(1)}, bf16[2048]{0:T(1024)(128)(2,1)}, u32[]{:S(2)}) copy-start(bf16[2048]{0:T(1024)(128)(2,1)} %param.14) | copy-start | bytes 12292
  61.1 53.4 %collective-permute-start.7 = (bf16[1024,512]{1,0:T(8,128)(2,1)}, bf16[1024,512]{1,0:T(8,128)(2,1)}, u32[]{:S(2)}, u32[]{:S(2)}) collective-permute-start(bf16[1024,512]{1,0:T(8,128)(2,1)} %get-tuple-element.63.refs_3_), channel_id=1, source_target_pairs={{0,2},{2,0},{1,3},{3,1},{4,6},{6,4},{5,7},{7,5}} | collective-permute-start | bytes 3145736 | tf_op jit(solution)/shard_map/ppermute | solution.py:485
  74.4 25.3 %copy-start.26 = (bf16[1024,512]{1,0:T(8,128)(2,1)}, bf16[1024,512]{1,0:T(8,128)(2,1)S(1)}, u32[]{:S(2)}) copy-start(bf16[1024,512]{1,0:T(8,128)(2,1)S(1)} %collective-permute-done.1) | copy-start | bytes 3145732
  74.4 26.6 %collective-permute-start.2 = (bf16[1024,512]{1,0:T(8,128)(2,1)S(1)}, bf16[1024,512]{1,0:T(8,128)(2,1)}, u32[]{:S(2)}, u32[]{:S(2)}) collective-permute-start(bf16[1024,512]{1,0:T(8,128)(2,1)S(1)} %collective-permute-done.1), channel_id=1, source_target_pairs={{0,1},{1,0},{2,3},{3,2},{4,5},{5,4},{6,7},{7,6}} | collective-permute-start | bytes 3145736 | tf_op jit(solution)/shard_map/ppermute | solution.py:482
  74.4 26.6 %collective-permute-start.5 = (bf16[512,2048]{1,0:T(8,128)(2,1)}, bf16[512,2048]{1,0:T(8,128)(2,1)}, u32[]{:S(2)}, u32[]{:S(2)}) collective-permute-start(bf16[512,2048]{1,0:T(8,128)(2,1)} %collective-permute-done.4.wc), channel_id=1, source_target_pairs={{0,1},{1,0},{2,3},{3,2},{4,5},{5,4},{6,7},{7,6}} | collective-permute-start | bytes 6291464 | tf_op jit(solution)/shard_map/ppermute | solution.py:482
  101.0 13.0 %copy-start.24 = (bf16[1024,512]{1,0:T(8,128)(2,1)S(1)}, bf16[1024,512]{1,0:T(8,128)(2,1)}, u32[]{:S(2)}) copy-start(bf16[1024,512]{1,0:T(8,128)(2,1)} %get-tuple-element.63.refs_3_) | copy-start | bytes 3145732
  113.9 21.4 %collective-permute-start.9 = (bf16[512,2048]{1,0:T(8,128)(2,1)}, bf16[512,2048]{1,0:T(8,128)(2,1)}, u32[]{:S(2)}, u32[]{:S(2)}) collective-permute-start(bf16[512,2048]{1,0:T(8,128)(2,1)} %get-tuple-element.69.own_n), channel_id=1, source_target_pairs={{0,1},{1,0},{2,3},{3,2},{4,5},{5,4},{6,7},{7,6}} | collective-permute-start | bytes 6291464 | tf_op jit(solution)/shard_map/ppermute | solution.py:482
  114.0 5.8 %collective-permute-start.6 = (bf16[1024,512]{1,0:T(8,128)(2,1)S(1)}, bf16[1024,512]{1,0:T(8,128)(2,1)S(1)}, u32[]{:S(2)}, u32[]{:S(2)}) collective-permute-start(bf16[1024,512]{1,0:T(8,128)(2,1)S(1)} %copy-done.24), channel_id=1, source_target_pairs={{0,1},{1,0},{2,3},{3,2},{4,5},{5,4},{6,7},{7,6}} | collective-permute-start | bytes 3145736 | tf_op jit(solution)/shard_map/ppermute | solution.py:482
  114.4 6.9 %collective-permute-start.8 = (bf16[1024,512]{1,0:T(8,128)(2,1)}, bf16[1024,512]{1,0:T(8,128)(2,1)S(1)}, u32[]{:S(2)}, u32[]{:S(2)}) collective-permute-start(bf16[1024,512]{1,0:T(8,128)(2,1)} %collective-permute-done.7), channel_id=1, source_target_pairs={{0,1},{1,0},{2,3},{3,2},{4,5},{5,4},{6,7},{7,6}} | collective-permute-start | bytes 3145736 | tf_op jit(solution)/shard_map/ppermute | solution.py:482
  135.2 36.0 %collective-permute-start.10 = (bf16[512,2048]{1,0:T(8,128)(2,1)}, bf16[512,2048]{1,0:T(8,128)(2,1)}, u32[]{:S(2)}, u32[]{:S(2)}) collective-permute-start(bf16[512,2048]{1,0:T(8,128)(2,1)} %get-tuple-element.72.own_n), channel_id=1, source_target_pairs={{0,1},{1,0},{2,3},{3,2},{4,5},{5,4},{6,7},{7,6}} | collective-permute-start | bytes 6291464 | tf_op jit(solution)/shard_map/ppermute | solution.py:482
  170.9 47.9 %collective-permute-start.11 = (bf16[512,2048]{1,0:T(8,128)(2,1)}, bf16[512,2048]{1,0:T(8,128)(2,1)S(1)}, u32[]{:S(2)}, u32[]{:S(2)}) collective-permute-start(bf16[512,2048]{1,0:T(8,128)(2,1)} %shard_map.142.sa), channel_id=1, source_target_pairs={{0,2},{2,0},{1,3},{3,1},{4,6},{6,4},{5,7},{7,5}} | collective-permute-start | bytes 6291464 | tf_op jit(solution)/shard_map/ppermute | solution.py:485
  191.8 27.0 %copy-start.7 = (bf16[1,2048]{1,0:T(2,128)(2,1)S(1)}, bf16[1,2048]{1,0:T(2,128)(2,1)}, u32[]{:S(2)}) copy-start(bf16[1,2048]{1,0:T(2,128)(2,1)} %broadcast_in_dim.4.g_ref) | copy-start | bytes 12292
  191.8 27.0 %copy-start.8 = (s32[2]{0:T(128)S(1)}, s32[2]{0:T(128)}, u32[]{:S(2)}) copy-start(s32[2]{0:T(128)} %pad_add_fusion.ids.refs_0_) | copy-start | bytes 28
  191.8 26.9 %copy-start.14 = (f32[512,2048]{1,0:T(8,128)S(1)}, f32[512,2048]{1,0:T(8,128)}, u32[]{:S(2)}) copy-start(f32[512,2048]{1,0:T(8,128)} %get-tuple-element.79.xh_ref) | copy-start | bytes 12582916
  191.8 26.9 %copy-start.16 = (bf16[512,2048]{1,0:T(8,128)(2,1)S(1)}, bf16[512,2048]{1,0:T(8,128)(2,1)}, u32[]{:S(2)}) copy-start(bf16[512,2048]{1,0:T(8,128)(2,1)} %shard_map.142.sa) | copy-start | bytes 6291460
  191.8 26.9 %copy-start.18 = (f32[512,128]{1,0:T(8,128)S(1)}, f32[512,128]{1,0:T(8,128)}, u32[]{:S(2)}) copy-start(f32[512,128]{1,0:T(8,128)} %get-tuple-element.80.rs_ref) | copy-start | bytes 786436
  225.1 2.0 copy-start
  227.1 15.7 %collective-permute-start.12 = (bf16[512,2048]{1,0:T(8,128)(2,1)}, bf16[512,2048]{1,0:T(8,128)(2,1)S(1)}, u32[]{:S(2)}, u32[]{:S(2)}) collective-permute-start(bf16[512,2048]{1,0:T(8,128)(2,1)} %get-tuple-element.81), channel_id=1, source_target_pairs={{0,1},{1,0},{2,3},{3,2},{4,5},{5,4},{6,7},{7,6}} | collective-permute-start | bytes 6291464 | tf_op jit(solution)/shard_map/ppermute | solution.py:482
  242.4 58.7 %collective-permute-start.13 = (bf16[512,2048]{1,0:T(8,128)(2,1)}, bf16[512,2048]{1,0:T(8,128)(2,1)}, u32[]{:S(2)}, u32[]{:S(2)}) collective-permute-start(bf16[512,2048]{1,0:T(8,128)(2,1)} %shard_map.145.sa), channel_id=1, source_target_pairs={{0,2},{2,0},{1,3},{3,1},{4,6},{6,4},{5,7},{7,5}} | collective-permute-start | bytes 6291464 | tf_op jit(solution)/shard_map/ppermute | solution.py:485
  242.8 2.2 copy-start.1
  246.1 3.8 copy-start.2
  288.7 12.4 %copy-start.9 = (s32[2]{0:T(128)S(1)}, s32[2]{0:T(128)}, u32[]{:S(2)}) copy-start(s32[2]{0:T(128)} %pad_add_fusion.ids.refs_0_) | copy-start | bytes 28
  288.8 12.4 %copy-start.17 = (f32[512,128]{1,0:T(8,128)S(1)}, f32[512,128]{1,0:T(8,128)}, u32[]{:S(2)}) copy-start(f32[512,128]{1,0:T(8,128)} %get-tuple-element.90.rs_ref) | copy-start | bytes 786436
  301.1 2.2 copy-start.13
  304.9 7.0 %copy-start.29 = (bf16[2048]{0:T(1024)(128)(2,1)S(1)}, bf16[2048]{0:T(1024)(128)(2,1)}, u32[]{:S(2)}) copy-start(bf16[2048]{0:T(1024)(128)(2,1)} %param.13) | copy-start | bytes 12292
  304.9 8.7 %copy-start.3 = (bf16[2,512,2048]{2,1,0:T(8,128)(2,1)S(1)}, bf16[2,512,2048]{2,1,0:T(8,128)(2,1)}, u32[]{:S(2)}) copy-start(bf16[2,512,2048]{2,1,0:T(8,128)(2,1)} %copy-done.2) | copy-start | bytes 12582916
  304.9 8.7 %copy-start.23 = (bf16[1024,512]{1,0:T(8,128)(2,1)S(1)}, bf16[1024,512]{1,0:T(8,128)(2,1)}, u32[]{:S(2)}) copy-start(bf16[1024,512]{1,0:T(8,128)(2,1)} %get-tuple-element.61.refs_3_) | copy-start | bytes 3145732
  311.6 6.4 %collective-permute-start.14 = (bf16[512,2048]{1,0:T(8,128)(2,1)S(1)}, bf16[512,2048]{1,0:T(8,128)(2,1)S(1)}, u32[]{:S(2)}, u32[]{:S(2)}) collective-permute-start(bf16[512,2048]{1,0:T(8,128)(2,1)S(1)} %get-tuple-element.91), channel_id=1, source_target_pairs={{0,1},{1,0},{2,3},{3,2},{4,5},{5,4},{6,7},{7,6}} | collective-permute-start | bytes 6291464 | tf_op jit(solution)/shard_map/ppermute | solution.py:482
  311.9 73.9 %collective-permute-start.15 = (bf16[512,2048]{1,0:T(8,128)(2,1)}, bf16[512,2048]{1,0:T(8,128)(2,1)S(1)}, u32[]{:S(2)}, u32[]{:S(2)}) collective-permute-start(bf16[512,2048]{1,0:T(8,128)(2,1)} %shard_map.148.sa), channel_id=1, source_target_pairs={{0,2},{2,0},{1,3},{3,1},{4,6},{6,4},{5,7},{7,5}} | collective-permute-start | bytes 6291464 | tf_op jit(solution)/shard_map/ppermute | solution.py:485
  318.7 4.2 copy-start.4
  341.9 12.8 %copy-start.25 = (bf16[1024,512]{1,0:T(8,128)(2,1)S(1)}, bf16[1024,512]{1,0:T(8,128)(2,1)}, u32[]{:S(2)}) copy-start(bf16[1024,512]{1,0:T(8,128)(2,1)} %get-tuple-element.63.refs_3_) | copy-start | bytes 3145732
  354.3 58.4 %collective-permute-start.16 = (bf16[512,2048]{1,0:T(8,128)(2,1)}, bf16[512,2048]{1,0:T(8,128)(2,1)S(1)}, u32[]{:S(2)}, u32[]{:S(2)}) collective-permute-start(bf16[512,2048]{1,0:T(8,128)(2,1)} %shard_map.152.sa), channel_id=1, source_target_pairs={{0,2},{2,0},{1,3},{3,1},{4,6},{6,4},{5,7},{7,5}} | collective-permute-start | bytes 6291464 | tf_op jit(solution)/shard_map/ppermute | solution.py:485
  354.7 31.1 %slice-start = ((s8[8388608]{0:T(1024)(128)(4,1)}), s8[4194304]{0:T(1024)(128)(4,1)S(1)}, s32[]{:S(2)}) async-start(s8[8388608]{0:T(1024)(128)(4,1)} %bitcast.39), calls=%async_computation | async-start | bytes 8388608
  362.0 23.8 %slice-start.1 = ((s8[8388608]{0:T(1024)(128)(4,1)}), s8[4194304]{0:T(1024)(128)(4,1)S(1)}, s32[]{:S(2)}) async-start(s8[8388608]{0:T(1024)(128)(4,1)} %bitcast.39), calls=%async_computation.1 | async-start | bytes 8388608
  362.0 23.9 %copy-start.10 = (s32[2]{0:T(128)S(1)}, s32[2]{0:T(128)}, u32[]{:S(2)}) copy-start(s32[2]{0:T(128)} %pad_add_fusion.ids.refs_0_) | copy-start | bytes 28
  362.0 23.9 %copy-start.11 = (f32[2048]{0:T(1024)S(1)}, f32[2048]{0:T(1024)}, u32[]{:S(2)}) copy-start(f32[2048]{0:T(1024)} %param.12) | copy-start | bytes 24580
  362.0 23.9 %copy-start.12 = (f32[2048]{0:T(1024)S(1)}, f32[2048]{0:T(1024)}, u32[]{:S(2)}) copy-start(f32[2048]{0:T(1024)} %param.11) | copy-start | bytes 24580
  362.0 23.9 %copy-start.19 = (f32[512,2048]{1,0:T(8,128)S(1)}, f32[512,2048]{1,0:T(8,128)}, u32[]{:S(2)}) copy-start(f32[512,2048]{1,0:T(8,128)} %get-tuple-element.105.dh_ref) | copy-start | bytes 12582916
  385.9 6.4 %copy-start.31 = (f32[2048]{0:T(1024)S(1)}, f32[2048]{0:T(1024)}, u32[]{:S(2)}) copy-start(f32[2048]{0:T(1024)} %copy-done.30) | copy-start | bytes 24580
  392.3 25.3 %collective-permute-start.18 = (bf16[512,2048]{1,0:T(8,128)(2,1)}, bf16[512,2048]{1,0:T(8,128)(2,1)S(1)}, u32[]{:S(2)}, u32[]{:S(2)}) collective-permute-start(bf16[512,2048]{1,0:T(8,128)(2,1)} %get-tuple-element.106), channel_id=1, source_target_pairs={{0,1},{1,0},{2,3},{3,2},{4,5},{5,4},{6,7},{7,6}} | collective-permute-start | bytes 6291464 | tf_op jit(solution)/shard_map/ppermute | solution.py:482
  392.4 20.4 %copy-start.5 = (f32[512,2048]{1,0:T(8,128)S(1)}, f32[512,2048]{1,0:T(8,128)}, u32[]{:S(2)}) copy-start(f32[512,2048]{1,0:T(8,128)} %get-tuple-element.109.dh_ref) | copy-start | bytes 12582916
  392.4 20.4 %copy-start.6 = (bf16[512,2048]{1,0:T(8,128)(2,1)S(1)}, bf16[512,2048]{1,0:T(8,128)(2,1)}, u32[]{:S(2)}) copy-start(bf16[512,2048]{1,0:T(8,128)(2,1)} %shard_map.152.sa) | copy-start | bytes 6291460
  417.1 4.2 collective-permute-start.17
  (6 other events, 7.8 us)
